TPU v7x, 256 devices: a whole 4x4x8 slice. The times are simulated.
256 devices in a mesh: grp: 16 (over x, y_hi, core), rng: 16 (over z, y_lo).
Axes of the slice: x: 4, y: 4 (y_hi: 2, y_lo: 2; y = y_hi * 2 + y_lo), z: 8, core: 2. Of those that a mesh axis runs over, the one named last changes fastest.
Arguments:
- features: bfloat16 [65536, 1024], P(('grp', 'rng')), may hold values from -6 to 6
- query_weight: bfloat16 [1024, 1024], replicated
- key_weight: bfloat16 [1024, 1024], replicated
- value_weight: bfloat16 [1024, 1024], replicated, may hold values from -0.1875 to 0.1875
- out_weight: bfloat16 [1024, 1024], replicated, may hold values from -0.1875 to 0.1875
- band_reach: int32 [256], P(('grp', 'rng')), may hold values from 16 to 128, as said below
- long_peers: int32 [512, 6], P(('grp', 'rng')), may hold values from 0 to 15, as said below
- long_count: int32 [512], P(('grp', 'rng')), may hold values from 0 to 6, as said below
- send_tile: int32 [256, 16], P(('grp', 'rng')), may hold values from 0 to 3
Outputs:
- updated: bfloat16 [65536, 1024], P(('grp', 'rng'))
Inputs may be any that keep to these rules, and one draw needn't show every extreme that they name: `band_reach`: some range has 128 in every draw. `long_peers`: the 6 entries of a query tile in region g are distinct regions other than g; only the first long_count entries are used. `long_count`: some query tile has 6 in every draw.
All inputs are finite; a program needn't handle non-finite values.
Results may differ from a plain program's by a relative error of at most 0.0064.
Values may be sent and summed in bfloat16 or wider, within the bound.
No kernel may reach another device: no remote copies, remote signals or barrier semaphores. Data moves between devices by JAX's collectives and lax.ppermute only.
A program may use at most 128 MiB of HBM per device.

v0:
```python
import jax
import jax.numpy as jnp
from jax import lax
from jax.experimental import pallas as pl
from jax.experimental.pallas import tpu as pltpu
from jax.sharding import PartitionSpec as P


TILE = 128
PORTAL = 64
MAXLONG = 6
EPSILON = 1e-06
LANES = 128
HEAD = 64
BLOCK = 256
PICKS = 8
EARLY = 9
LATE = 6
MIB = 1024 * 1024
SCALE2 = HEAD**-0.5 * 1.4426950408889634
F32 = jnp.float32
BF16 = jnp.bfloat16

VMEM = pl.BlockSpec(memory_space=pltpu.VMEM)
SMEM = pl.BlockSpec(memory_space=pltpu.SMEM)


def region(x, y, c):
    return (x % 4) * 4 + (y % 2) * 2 + c % 2


def moved(dx, dy, dc):
    return [
        (region(x, y, c), region(x + dx, y + dy, c ^ dc))
        for x in range(4)
        for y in range(2)
        for c in range(2)
    ]


def place_of(index):
    return index // 4, (index // 2) % 2, index % 2


def pack_kernel(send_ref, feat_ref, a_ref, x1_ref, x2_ref, x3_ref, up_ref, down_ref, mate_ref):
    rows = feat_ref.shape[0]
    widened = feat_ref[...].astype(F32)
    factor = lax.rsqrt(jnp.mean(widened * widened, axis=1, keepdims=True) + EPSILON)
    normed = (widened * factor).astype(BF16)
    a_ref[:rows] = normed
    down_ref[...] = normed[:TILE]
    up_ref[...] = normed[rows - TILE :]
    x, y, c = place_of(lax.axis_index("grp"))

    def tile(dx, dy, dc):
        pick = send_ref[0, ((x + dx) % 4) * 4 + (y ^ dy) * 2 + (c ^ dc)]
        return pick

    def rows_of(pick):
        return a_ref[pl.ds(pl.multiple_of(pick * PORTAL, PORTAL), PORTAL)]

    for dx, ref in ((1, x1_ref), (2, x2_ref), (3, x3_ref)):
        for dc in range(2):
            ref[dc * PORTAL : (dc + 1) * PORTAL] = rows_of(tile(dx, 0, dc))
    mate_ref[...] = rows_of(tile(0, 0, 1))
    row = lax.broadcasted_iota(jnp.int32, (PICKS, feat_ref.shape[1]), 0)
    picks = jnp.zeros(row.shape, jnp.int32)
    for i in range(PICKS):
        picks = jnp.where(row == i, tile(i // 2, 1, i % 2), picks)
    a_ref[rows:] = picks.astype(F32).astype(BF16)


def relay_kernel(a_ref, *out_refs):
    rows = a_ref.shape[0] - PICKS
    picks = a_ref[rows:].astype(F32)
    for i, ref in enumerate(out_refs):
        pick = jnp.broadcast_to(picks[i : i + 1], (PORTAL, picks.shape[1]))
        tile = a_ref[:PORTAL].astype(F32)
        for k in range(1, rows // PORTAL):
            tile = jnp.where(
                pick == float(k), a_ref[k * PORTAL : (k + 1) * PORTAL].astype(F32), tile
            )
        ref[...] = tile.astype(BF16)


def dot(x, w):
    return jnp.dot(x, w, preferred_element_type=F32)


def local_kernel(a_ref, wq_ref, wk_ref, wv_ref, q_ref, k_ref, v_ref):
    rows = q_ref.shape[0]
    normed = a_ref[:rows]
    q_ref[...] = dot(normed, wq_ref[...]).astype(BF16)
    k_ref[...] = dot(normed, wk_ref[...]).astype(BF16)
    v_ref[...] = dot(normed, wv_ref[...]).astype(BF16)


def low_lanes():
    return lax.broadcasted_iota(jnp.int32, (TILE, LANES), 1) < HEAD


def pair_queries(q):
    low = low_lanes()
    zero = jnp.zeros_like(q)
    return jnp.concatenate([jnp.where(low, q, zero), jnp.where(low, zero, q)], axis=0)


def unpair(x):
    x = jnp.broadcast_to(x, (2 * TILE, LANES))
    return jnp.where(low_lanes(), x[:TILE], x[TILE:])


def pair_scores(q, k):
    return lax.dot_general(
        pair_queries(q), k, (((1,), (1,)), ((), ())), preferred_element_type=F32
    )


def band_kernel(
    reach_ref, q_ref, k_ref, v_ref, lo_ref, hi_ref, wk_ref, wv_ref,
    acc_ref, max_ref, sum_ref, x_s, k_s, v_s, bias_s,
):
    rows = q_ref.shape[0]

    @pl.when(pl.program_id(0) == 0)
    def _():
        x_s[:TILE] = lo_ref[...]
        x_s[TILE:] = hi_ref[...]
        place = lax.broadcasted_iota(jnp.int32, bias_s.shape, 0) % TILE
        key = lax.broadcasted_iota(jnp.int32, bias_s.shape, 1)
        inside = jnp.abs(place + TILE - key) <= reach_ref[0]
        bias_s[...] = jnp.where(inside, 0.0, -jnp.inf)

    for w_ref, here_ref, ext in ((wk_ref, k_ref, k_s), (wv_ref, v_ref, v_s)):
        rim = dot(x_s[...], w_ref[...]).astype(BF16)
        ext[:TILE] = rim[:TILE]
        ext[TILE : TILE + rows] = here_ref[...]
        ext[TILE + rows :] = rim[TILE:]
    for h in range(q_ref.shape[1] // LANES):
        cols = slice(h * LANES, (h + 1) * LANES)
        for t in range(rows // TILE):
            here = slice(t * TILE, (t + 1) * TILE)
            keys = slice(t * TILE, (t + 3) * TILE)
            s = pair_scores(q_ref[here, cols], k_s[keys, cols]) * SCALE2 + bias_s[...]
            m = jnp.max(s, axis=1, keepdims=True)
            p = jnp.exp2(s - m)
            acc = dot(p.astype(BF16), v_s[keys, cols])
            max_ref[here, cols] = unpair(m)
            sum_ref[here, cols] = unpair(jnp.sum(p, axis=1, keepdims=True))
            acc_ref[here, cols] = unpair(acc)


def early_kernel(*refs):
    (_, mine_ref, x1_ref, x2_ref, x3_ref, swap_ref, wk_ref, wv_ref, k_ref, v_ref, x_s) = refs

    @pl.when(pl.program_id(0) == 0)
    def _():
        def put(pos, ref, start):
            x_s[(pos - 1) * PORTAL : pos * PORTAL] = ref[start * PORTAL : (start + 1) * PORTAL]

        put(8, mine_ref, 0)
        for dx, ref in ((1, x1_ref), (2, x2_ref), (3, x3_ref)):
            put(2 * dx, ref, 0)
        for i, pos in enumerate((1, 9, 3, 5, 7)):
            put(pos, swap_ref, i)

    k_ref[...] = dot(x_s[...], wk_ref[...]).astype(BF16)
    v_ref[...] = dot(x_s[...], wv_ref[...]).astype(BF16)


def late_kernel(
    peers_ref, count_ref, q_ref, acc_ref, max_ref, sum_ref, feat_ref, ke_ref, ve_ref,
    l0, l1, l2, l3, l4, l5, wk_ref, wv_ref, wo_ref, out_ref, x_s, k_s, v_s, out_s,
):
    rows = q_ref.shape[0]
    span = MAXLONG * PORTAL
    step = pl.program_id(0)

    @pl.when(step == 0)
    def _():
        for i, ref in enumerate((l0, l1, l2, l3, l4, l5)):
            x_s[i * PORTAL : (i + 1) * PORTAL] = ref[...]

    split = EARLY * PORTAL
    k_s[:split] = ke_ref[...]
    v_s[:split] = ve_ref[...]
    k_s[split:] = dot(x_s[...], wk_ref[...]).astype(BF16)
    v_s[split:] = dot(x_s[...], wv_ref[...]).astype(BF16)
    x, y, c = place_of(lax.axis_index("grp"))
    slot = lax.broadcasted_iota(jnp.int32, (1, span), 1) // PORTAL
    attended = []
    for h in range(q_ref.shape[1] // LANES):
        cols = slice(h * LANES, (h + 1) * LANES)
        tiles = []
        for t in range(rows // TILE):
            here = slice(t * TILE, (t + 1) * TILE)
            starts = []
            for s in range(MAXLONG):
                px, py, pc = place_of(peers_ref[t, s])
                pos = (y ^ py) * 8 + ((x - px + 4) % 4) * 2 + (c ^ pc)
                starts.append(pl.multiple_of((pos - 1) * PORTAL, PORTAL))
            keys = jnp.concatenate([k_s[pl.ds(i, PORTAL), cols] for i in starts], axis=0)
            values = jnp.concatenate([v_s[pl.ds(i, PORTAL), cols] for i in starts], axis=0)
            bias = jnp.where(slot < count_ref[t], 0.0, -jnp.inf)
            s = pair_scores(q_ref[here, cols], keys) * SCALE2 + bias
            band_max = max_ref[here, cols]
            band_max = jnp.concatenate(
                [band_max[:, :1], band_max[:, HEAD : HEAD + 1]], axis=0
            )
            m = jnp.maximum(jnp.max(s, axis=1, keepdims=True), band_max)
            p = jnp.exp2(s - m)
            acc = unpair(dot(p.astype(BF16), values))
            total = unpair(jnp.sum(p, axis=1, keepdims=True))
            keep = unpair(jnp.exp2(band_max - m))
            acc = acc + keep * acc_ref[here, cols]
            total = total + keep * sum_ref[here, cols]
            tiles.append((acc / total).astype(BF16))
        attended.append(jnp.concatenate(tiles, axis=0))
    part = dot(jnp.concatenate(attended, axis=1), wo_ref[...])

    @pl.when(step == 0)
    def _():
        out_s[...] = feat_ref[...].astype(F32) + part

    @pl.when(step > 0)
    def _():
        out_s[...] = out_s[...] + part

    @pl.when(step == pl.num_programs(0) - 1)
    def _():
        out_ref[...] = out_s[...].astype(BF16)


def named(kernel, **kw):
    def run(*args):
        return pl.pallas_call(kernel, **kw)(*args)

    return run


def shape(*dims, dtype=BF16):
    return jax.ShapeDtypeStruct(dims, dtype)


def cols_of(rows, block=BLOCK):
    return pl.BlockSpec((rows, block), lambda i: (0, i))


def whole(rows, width):
    return pl.BlockSpec((rows, width), lambda i: (0, 0))


def params(mib):
    return pltpu.CompilerParams(vmem_limit_bytes=mib * MIB)


def local(
    features, query_weight, key_weight, value_weight, out_weight,
    band_reach, long_peers, long_count, send_tile,
):
    rows, width = features.shape
    ranks = lax.axis_size("rng")
    steps = width // BLOCK
    tall = shape(2 * PORTAL, width)
    half = shape(TILE, width)
    tile = shape(PORTAL, width)
    a, x1, x2, x3, up, down, mate = named(pack_kernel,
        out_shape=(shape(rows + PICKS, width), tall, tall, tall, half, half, tile),
        in_specs=[SMEM, VMEM],
        out_specs=(VMEM,) * 7,
        compiler_params=params(8),
    )(send_tile, features)
    across = lax.ppermute(a, "grp", moved(0, 1, 0))
    x1, x2, x3 = [
        lax.ppermute(part, "grp", moved(dx, 0, 0))
        for dx, part in ((1, x1), (2, x2), (3, x3))
    ]
    lo = lax.ppermute(up, "rng", [(i, (i + 1) % ranks) for i in range(ranks)])
    hi = lax.ppermute(down, "rng", [(i, (i - 1) % ranks) for i in range(ranks)])
    square = shape(rows, width)
    w_cols = cols_of(width)
    queries, keys, values = named(local_kernel,
        grid=(steps,),
        out_shape=(square,) * 3,
        in_specs=[whole(rows + PICKS, width)] + [w_cols] * 3,
        out_specs=(cols_of(rows),) * 3,
        compiler_params=params(16),
    )(a, query_weight, key_weight, value_weight)
    relayed = named(relay_kernel,
        out_shape=(tile,) * PICKS,
        in_specs=[VMEM],
        out_specs=(VMEM,) * PICKS,
        compiler_params=params(8),
    )(across)
    late = [lax.ppermute(relayed[i], "grp", moved(i // 2, 0, i % 2)) for i in range(2, PICKS)]
    swapped = lax.ppermute(
        jnp.concatenate([mate, relayed[1], x1[PORTAL:], x2[PORTAL:], x3[PORTAL:]], axis=0),
        "grp",
        moved(0, 0, 1),
    )
    wide = shape(rows, width, dtype=F32)
    acc, top, total = named(band_kernel,
        grid=(steps,),
        out_shape=(wide,) * 3,
        in_specs=[SMEM] + [cols_of(rows)] * 3 + [whole(TILE, width)] * 2 + [w_cols] * 2,
        out_specs=(cols_of(rows),) * 3,
        scratch_shapes=[
            pltpu.VMEM((2 * TILE, width), BF16),
            pltpu.VMEM((rows + 2 * TILE, BLOCK), BF16),
            pltpu.VMEM((rows + 2 * TILE, BLOCK), BF16),
            pltpu.VMEM((2 * TILE, 3 * TILE), F32),
        ],
        compiler_params=params(16),
    )(band_reach, queries, keys, values, lo, hi, key_weight, value_weight)
    early_rows = EARLY * PORTAL
    early_keys, early_values = named(early_kernel,
        grid=(steps,),
        out_shape=(shape(early_rows, width),) * 2,
        in_specs=[whole(PORTAL, width)] * 2
        + [whole(2 * PORTAL, width)] * 3
        + [whole(5 * PORTAL, width)]
        + [w_cols] * 2,
        out_specs=(cols_of(early_rows),) * 2,
        scratch_shapes=[pltpu.VMEM((early_rows, width), BF16)],
        compiler_params=params(16),
    )(mate, relayed[0], x1, x2, x3, swapped, key_weight, value_weight)
    late_rows = LATE * PORTAL
    return named(late_kernel,
        grid=(steps,),
        out_shape=square,
        in_specs=[SMEM, SMEM]
        + [cols_of(rows)] * 4
        + [whole(rows, width)]
        + [cols_of(early_rows)] * 2
        + [whole(PORTAL, width)] * LATE
        + [w_cols] * 2
        + [pl.BlockSpec((BLOCK, width), lambda i: (i, 0))],
        out_specs=whole(rows, width),
        scratch_shapes=[
            pltpu.VMEM((late_rows, width), BF16),
            pltpu.VMEM((early_rows + late_rows, BLOCK), BF16),
            pltpu.VMEM((early_rows + late_rows, BLOCK), BF16),
            pltpu.VMEM((rows, width), F32),
        ],
        compiler_params=params(20),
    )(
        long_peers, long_count, queries, acc, top, total, features, early_keys, early_values,
        *late, key_weight, value_weight, out_weight,
    )


def solution(mesh):
    spread = ("grp", "rng")
    return jax.shard_map(
        local,
        mesh=mesh,
        in_specs=(
            P(spread, None), P(), P(), P(), P(),
            P(spread), P(spread, None), P(spread), P(spread, None),
        ),
        out_specs=P(spread, None),
        check_vma=False,
    )
```

profile of v0, /device:TPU:1, one launch (start us, length us, event | category | flops | bytes accessed | tf_op | source)
XLA Modules:
  0.0 75.3 jit_solution(17677287193499358739)
XLA Ops:
  0.0 1.2 %copy-done.3 = bf16[256,1024]{1,0:T(8,128)(2,1)S(1)} copy-done((bf16[256,1024]{1,0:T(8,128)(2,1)S(1)}, bf16[256,1024]{1,0:T(8,128)(2,1)}, u32[]{:S(2)}) %copy-start.3) | copy-done | bytes 524312
  1.2 0.7 copy-done.8
  1.9 0.8 %shard_map.91 = (bf16[264,1024]{1,0:T(8,128)(2,1)S(1)}, bf16[128,1024]{1,0:T(8,128)(2,1)S(1)}, bf16[128,1024]{1,0:T(8,128)(2,1)S(1)}, bf16[128,1024]{1,0:T(8,128...) custom-call(s32[1,16]{1,0:T(1,128)S(1)} %copy-done.8, ...), custom_call_target="tpu_custom_call" | custom-call | tf_op jit(solution)/shard_map/pallas_call | solution.py:236
  2.7 3.8 %collective-permute-start.2 = (bf16[264,1024]{1,0:T(8,128)(2,1)S(1)}, bf16[264,1024]{1,0:T(8,128)(2,1)S(1)}, u32[]{:S(2)}, u32[]{:S(2)}) collective-permute-start(bf16[264,1024]{1,0:T(8,128)(2,1)S(1)} %get-tuple-element.28.a_ref), channel_id=1, source_target_pairs={{0,32},{16,48},{32,0},{48,16},{64,96},{80,112},{96,64},{112,80},{1... | collective-permute-start | bytes 1622024 | tf_op jit(solution)/shard_map/ppermute | solution.py:273
  6.5 1.2 %collective-permute-start.3 = (bf16[128,1024]{1,0:T(8,128)(2,1)S(1)}, bf16[128,1024]{1,0:T(8,128)(2,1)S(1)}, u32[]{:S(2)}, u32[]{:S(2)}) collective-permute-start(bf16[128,1024]{1,0:T(8,128)(2,1)S(1)} %get-tuple-element.39), channel_id=1, source_target_pairs={{0,64},{16,80},{32,96},{48,112},{64,128},{80,144},{96,160},{112,17... | collective-permute-start | bytes 786440 | tf_op jit(solution)/shard_map/ppermute | solution.py:275
  7.7 2.5 %collective-permute-start.4 = (bf16[128,1024]{1,0:T(8,128)(2,1)S(1)}, bf16[128,1024]{1,0:T(8,128)(2,1)S(1)}, u32[]{:S(2)}, u32[]{:S(2)}) collective-permute-start(bf16[128,1024]{1,0:T(8,128)(2,1)S(1)} %get-tuple-element.40), channel_id=1, source_target_pairs={{0,128},{16,144},{32,160},{48,176},{64,192},{80,208},{96,224},{112... | collective-permute-start | bytes 786440 | tf_op jit(solution)/shard_map/ppermute | solution.py:275
  10.1 1.2 %collective-permute-start.5 = (bf16[128,1024]{1,0:T(8,128)(2,1)S(1)}, bf16[128,1024]{1,0:T(8,128)(2,1)S(1)}, u32[]{:S(2)}, u32[]{:S(2)}) collective-permute-start(bf16[128,1024]{1,0:T(8,128)(2,1)S(1)} %get-tuple-element.41), channel_id=1, source_target_pairs={{0,192},{16,208},{32,224},{48,240},{64,0},{80,16},{96,32},{112,48}... | collective-permute-start | bytes 786440 | tf_op jit(solution)/shard_map/ppermute | solution.py:275
  11.3 6.1 %collective-permute-done.2.a_ref = bf16[264,1024]{1,0:T(8,128)(2,1)S(1)} collective-permute-done((bf16[264,1024]{1,0:T(8,128)(2,1)S(1)}, bf16[264,1024]{1,0:T(8,128)(2,1)S(1)}, u32[]{:S(2)}, u32[]{:S(2)}) %collective-permute-start.2) | collective-permute-done | bytes 540704 | tf_op jit(solution)/shard_map/ppermute | solution.py:273
  17.4 0.6 shard_map.94
  18.1 3.1 %collective-permute-done.4.refs_3_ = bf16[128,1024]{1,0:T(8,128)(2,1)S(1)} collective-permute-done((bf16[128,1024]{1,0:T(8,128)(2,1)S(1)}, bf16[128,1024]{1,0:T(8,128)(2,1)S(1)}, u32[]{:S(2)}, u32[]{:S(2)}) %collective-permute-start.4) | collective-permute-done | bytes 262176 | tf_op jit(solution)/shard_map/ppermute | solution.py:275
  21.2 1.9 %collective-permute-start.6 = (bf16[320,1024]{1,0:T(8,128)(2,1)S(1)}, bf16[320,1024]{1,0:T(8,128)(2,1)S(1)}, u32[]{:S(2)}, u32[]{:S(2)}) collective-permute-start(bf16[320,1024]{1,0:T(8,128)(2,1)S(1)} %slice_dynamic-update-slice_fusion), channel_id=1, source_target_pairs={{0,16},{16,0},{32,48},{48,32},{64,80},{80,64},{96,112},{112,96},{1... | collective-permute-start | bytes 1966088 | tf_op jit(solution)/shard_map/ppermute | solution.py:296
  23.1 0.4 collective-permute-start
  23.5 5.3 %collective-permute-start.1 = (bf16[128,1024]{1,0:T(8,128)(2,1)S(1)}, bf16[128,1024]{1,0:T(8,128)(2,1)S(1)}, u32[]{:S(2)}, u32[]{:S(2)}) collective-permute-start(bf16[128,1024]{1,0:T(8,128)(2,1)S(1)} %get-tuple-element.33), channel_id=1, source_target_pairs={{0,15},{1,0},{2,1},{3,2},{4,3},{5,4},{6,5},{7,6},{8,7},{9,8},{10,9... | collective-permute-start | bytes 786440 | tf_op jit(solution)/shard_map/ppermute | solution.py:279
  28.8 1.0 %collective-permute-start.7 = (bf16[64,1024]{1,0:T(8,128)(2,1)S(1)}, bf16[64,1024]{1,0:T(8,128)(2,1)S(1)}, u32[]{:S(2)}, u32[]{:S(2)}) collective-permute-start(bf16[64,1024]{1,0:T(8,128)(2,1)S(1)} %get-tuple-element.45), channel_id=1, source_target_pairs={{0,64},{16,80},{32,96},{48,112},{64,128},{80,144},{96,160},{112,17... | collective-permute-start | bytes 393224 | tf_op jit(solution)/shard_map/ppermute | solution.py:295
  29.9 1.6 %collective-permute-start.8 = (bf16[64,1024]{1,0:T(8,128)(2,1)S(1)}, bf16[64,1024]{1,0:T(8,128)(2,1)S(1)}, u32[]{:S(2)}, u32[]{:S(2)}) collective-permute-start(bf16[64,1024]{1,0:T(8,128)(2,1)S(1)} %get-tuple-element.46), channel_id=1, source_target_pairs={{0,80},{16,64},{32,112},{48,96},{64,144},{80,128},{96,176},{112,16... | collective-permute-start | bytes 393224 | tf_op jit(solution)/shard_map/ppermute | solution.py:295
  31.5 4.0 %collective-permute-done.lo_ref = bf16[128,1024]{1,0:T(8,128)(2,1)S(1)} collective-permute-done((bf16[128,1024]{1,0:T(8,128)(2,1)S(1)}, bf16[128,1024]{1,0:T(8,128)(2,1)S(1)}, u32[]{:S(2)}, u32[]{:S(2)}) %collective-permute-start) | collective-permute-done | bytes 262176 | tf_op jit(solution)/shard_map/ppermute | solution.py:278
  35.5 2.4 %collective-permute-start.9 = (bf16[64,1024]{1,0:T(8,128)(2,1)S(1)}, bf16[64,1024]{1,0:T(8,128)(2,1)S(1)}, u32[]{:S(2)}, u32[]{:S(2)}) collective-permute-start(bf16[64,1024]{1,0:T(8,128)(2,1)S(1)} %get-tuple-element.47), channel_id=1, source_target_pairs={{0,128},{16,144},{32,160},{48,176},{64,192},{80,208},{96,224},{112... | collective-permute-start | bytes 393224 | tf_op jit(solution)/shard_map/ppermute | solution.py:295
  37.8 0.1 collective-permute-done.1.hi_ref
  37.9 3.2 %collective-permute-start.10 = (bf16[64,1024]{1,0:T(8,128)(2,1)S(1)}, bf16[64,1024]{1,0:T(8,128)(2,1)S(1)}, u32[]{:S(2)}, u32[]{:S(2)}) collective-permute-start(bf16[64,1024]{1,0:T(8,128)(2,1)S(1)} %get-tuple-element.48), channel_id=1, source_target_pairs={{0,144},{16,128},{32,176},{48,160},{64,208},{80,192},{96,240},{112... | collective-permute-start | bytes 393224 | tf_op jit(solution)/shard_map/ppermute | solution.py:295
  41.1 1.1 %collective-permute-start.11 = (bf16[64,1024]{1,0:T(8,128)(2,1)S(1)}, bf16[64,1024]{1,0:T(8,128)(2,1)S(1)}, u32[]{:S(2)}, u32[]{:S(2)}) collective-permute-start(bf16[64,1024]{1,0:T(8,128)(2,1)S(1)} %get-tuple-element.49), channel_id=1, source_target_pairs={{0,192},{16,208},{32,224},{48,240},{64,0},{80,16},{96,32},{112,48}... | collective-permute-start | bytes 393224 | tf_op jit(solution)/shard_map/ppermute | solution.py:295
  42.1 0.0 collective-permute-start.12
  42.8 0.0 copy-start.1
  42.8 1.6 %copy-done.1 = bf16[1024,1024]{1,0:T(8,128)(2,1)S(1)} copy-done((bf16[1024,1024]{1,0:T(8,128)(2,1)S(1)}, bf16[1024,1024]{1,0:T(8,128)(2,1)}, u32[]{:S(2)}) %copy-start.1) | copy-done | bytes 2097176
  44.4 1.6 %copy-done.5 = bf16[1024,1024]{1,0:T(8,128)(2,1)S(1)} copy-done((bf16[1024,1024]{1,0:T(8,128)(2,1)S(1)}, bf16[1024,1024]{1,0:T(8,128)(2,1)}, u32[]{:S(2)}) %copy-start.5) | copy-done | bytes 2097176
  46.0 3.3 %shard_map.92 = (bf16[256,1024]{1,0:T(8,128)(2,1)S(1)}, bf16[256,1024]{1,0:T(8,128)(2,1)S(1)}, bf16[256,1024]{1,0:T(8,128)(2,1)S(1)}) custom-call(bf16[264,1024]{1,0:T(8,128)(2,1)S(1)} %get-tuple-element.28.a_ref, bf16[1024,1024]{1,0:T(8,128)(2,1)S(1)} %copy-done.5, bf16[1024,1024]{1,0:T(8,128)(2,1)S(1)} %copy-done, bf16[1024,1024]{1,0:T(8,128)(2,1)S(1)} %copy-done.1), custom_call_target="tpu_custom_call" | custom-call | tf_op jit(solution)/shard_map/pallas_call | solution.py:236
  49.4 8.0 %shard_map.93 = (f32[256,1024]{1,0:T(8,128)S(1)}, f32[256,1024]{1,0:T(8,128)S(1)}, f32[256,1024]{1,0:T(8,128)S(1)}) custom-call(s32[1]{0:T(128)S(6)} %copy.14.reach_ref, bf16[256,1024]{1,0:T(8,128)(2,1)S(1)} %get-tuple-element.29.q_ref, bf16[256,1024]{1,0:T(8,128)(2,1)S(1)} %get-tuple-element.30.k_ref, bf16[256,1024]{1,0:T(8,128)(2,1)S(1)} %get-tuple-element.31.v_ref, ...), custom_call_target="tpu_custom_call" | custom-call | tf_op jit(solution)/shard_map/pallas_call | solution.py:236
  57.4 0.0 copy-start.4
  57.4 0.0 copy-start.6
  57.4 0.0 copy-start.7
  57.4 0.0 copy-start.9
  57.4 4.1 %shard_map.95 = (bf16[576,1024]{1,0:T(8,128)(2,1)S(1)}, bf16[576,1024]{1,0:T(8,128)(2,1)S(1)}) custom-call(bf16[64,1024]{1,0:T(8,128)(2,1)S(1)} %get-tuple-element.37.refs_0_, bf16[64,1024]{1,0:T(8,128)(2,1)S(1)} %get-tuple-element.38.refs_1_, bf16[128,1024]{1,0:T(8,128)(2,1)S(1)} %collective-permute-done.3.refs_2_, ...), custom_call_target="tpu_custom_call" | custom-call | tf_op jit(solution)/shard_map/pallas_call | solution.py:236
  61.6 13.7 %shard_map.96 = bf16[256,1024]{1,0:T(8,128)(2,1)} custom-call(s32[2,6]{1,0:T(2,128)S(1)} %copy-done.7, s32[2]{0:T(128)S(1)} %copy-done.9, bf16[256,1024]{1,0:T(8,128)(2,1)S(1)} %get-tuple-element.29.q_ref, f32[256,1024]{1,0:T(8,128)S(1)} %get-tuple-element.34.acc_ref, f32[256,1024]{1,0:T(8,128)S(1)} %get-tuple-element.35.max_ref, ...), custom_call_target="tpu_custom_call" | custom-call | tf_op jit(solution)/shard_map/pallas_call | solution.py:236
  (25 shorter events, 0.1 us)
Async XLA Ops:
  0.0 42.8 %copy-start = (bf16[1024,1024]{1,0:T(8,128)(2,1)S(1)}, bf16[1024,1024]{1,0:T(8,128)(2,1)}, u32[]{:S(2)}) copy-start(bf16[1024,1024]{1,0:T(8,128)(2,1)} %wk_ref.5) | copy-start | bytes 6291460
  0.0 1.2 %copy-start.3 = (bf16[256,1024]{1,0:T(8,128)(2,1)S(1)}, bf16[256,1024]{1,0:T(8,128)(2,1)}, u32[]{:S(2)}) copy-start(bf16[256,1024]{1,0:T(8,128)(2,1)} %feat_ref.3) | copy-start | bytes 1572868
  1.2 0.7 copy-start.8
  2.7 14.8 %collective-permute-start.2 = (bf16[264,1024]{1,0:T(8,128)(2,1)S(1)}, bf16[264,1024]{1,0:T(8,128)(2,1)S(1)}, u32[]{:S(2)}, u32[]{:S(2)}) collective-permute-start(bf16[264,1024]{1,0:T(8,128)(2,1)S(1)} %get-tuple-element.28.a_ref), channel_id=1, source_target_pairs={{0,32},{16,48},{32,0},{48,16},{64,96},{80,112},{96,64},{112,80},{1... | collective-permute-start | bytes 1622024 | tf_op jit(solution)/shard_map/ppermute | solution.py:273
  6.5 11.6 %collective-permute-start.3 = (bf16[128,1024]{1,0:T(8,128)(2,1)S(1)}, bf16[128,1024]{1,0:T(8,128)(2,1)S(1)}, u32[]{:S(2)}, u32[]{:S(2)}) collective-permute-start(bf16[128,1024]{1,0:T(8,128)(2,1)S(1)} %get-tuple-element.39), channel_id=1, source_target_pairs={{0,64},{16,80},{32,96},{48,112},{64,128},{80,144},{96,160},{112,17... | collective-permute-start | bytes 786440 | tf_op jit(solution)/shard_map/ppermute | solution.py:275
  7.7 13.5 %collective-permute-start.4 = (bf16[128,1024]{1,0:T(8,128)(2,1)S(1)}, bf16[128,1024]{1,0:T(8,128)(2,1)S(1)}, u32[]{:S(2)}, u32[]{:S(2)}) collective-permute-start(bf16[128,1024]{1,0:T(8,128)(2,1)S(1)} %get-tuple-element.40), channel_id=1, source_target_pairs={{0,128},{16,144},{32,160},{48,176},{64,192},{80,208},{96,224},{112... | collective-permute-start | bytes 786440 | tf_op jit(solution)/shard_map/ppermute | solution.py:275
  10.1 11.1 %collective-permute-start.5 = (bf16[128,1024]{1,0:T(8,128)(2,1)S(1)}, bf16[128,1024]{1,0:T(8,128)(2,1)S(1)}, u32[]{:S(2)}, u32[]{:S(2)}) collective-permute-start(bf16[128,1024]{1,0:T(8,128)(2,1)S(1)} %get-tuple-element.41), channel_id=1, source_target_pairs={{0,192},{16,208},{32,224},{48,240},{64,0},{80,16},{96,32},{112,48}... | collective-permute-start | bytes 786440 | tf_op jit(solution)/shard_map/ppermute | solution.py:275
  21.2 20.9 %collective-permute-start.6 = (bf16[320,1024]{1,0:T(8,128)(2,1)S(1)}, bf16[320,1024]{1,0:T(8,128)(2,1)S(1)}, u32[]{:S(2)}, u32[]{:S(2)}) collective-permute-start(bf16[320,1024]{1,0:T(8,128)(2,1)S(1)} %slice_dynamic-update-slice_fusion), channel_id=1, source_target_pairs={{0,16},{16,0},{32,48},{48,32},{64,80},{80,64},{96,112},{112,96},{1... | collective-permute-start | bytes 1966088 | tf_op jit(solution)/shard_map/ppermute | solution.py:296
  23.1 12.3 %collective-permute-start = (bf16[128,1024]{1,0:T(8,128)(2,1)S(1)}, bf16[128,1024]{1,0:T(8,128)(2,1)S(1)}, u32[]{:S(2)}, u32[]{:S(2)}) collective-permute-start(bf16[128,1024]{1,0:T(8,128)(2,1)S(1)} %get-tuple-element.32), channel_id=1, source_target_pairs={{0,1},{1,2},{2,3},{3,4},{4,5},{5,6},{6,7},{7,8},{8,9},{9,10},{10,1... | collective-permute-start | bytes 786440 | tf_op jit(solution)/shard_map/ppermute | solution.py:278
  23.5 14.3 %collective-permute-start.1 = (bf16[128,1024]{1,0:T(8,128)(2,1)S(1)}, bf16[128,1024]{1,0:T(8,128)(2,1)S(1)}, u32[]{:S(2)}, u32[]{:S(2)}) collective-permute-start(bf16[128,1024]{1,0:T(8,128)(2,1)S(1)} %get-tuple-element.33), channel_id=1, source_target_pairs={{0,15},{1,0},{2,1},{3,2},{4,3},{5,4},{6,5},{7,6},{8,7},{9,8},{10,9... | collective-permute-start | bytes 786440 | tf_op jit(solution)/shard_map/ppermute | solution.py:279
  28.8 12.2 %collective-permute-start.7 = (bf16[64,1024]{1,0:T(8,128)(2,1)S(1)}, bf16[64,1024]{1,0:T(8,128)(2,1)S(1)}, u32[]{:S(2)}, u32[]{:S(2)}) collective-permute-start(bf16[64,1024]{1,0:T(8,128)(2,1)S(1)} %get-tuple-element.45), channel_id=1, source_target_pairs={{0,64},{16,80},{32,96},{48,112},{64,128},{80,144},{96,160},{112,17... | collective-permute-start | bytes 393224 | tf_op jit(solution)/shard_map/ppermute | solution.py:295
  29.9 31.6 %collective-permute-start.8 = (bf16[64,1024]{1,0:T(8,128)(2,1)S(1)}, bf16[64,1024]{1,0:T(8,128)(2,1)S(1)}, u32[]{:S(2)}, u32[]{:S(2)}) collective-permute-start(bf16[64,1024]{1,0:T(8,128)(2,1)S(1)} %get-tuple-element.46), channel_id=1, source_target_pairs={{0,80},{16,64},{32,112},{48,96},{64,144},{80,128},{96,176},{112,16... | collective-permute-start | bytes 393224 | tf_op jit(solution)/shard_map/ppermute | solution.py:295
  35.5 26.0 %collective-permute-start.9 = (bf16[64,1024]{1,0:T(8,128)(2,1)S(1)}, bf16[64,1024]{1,0:T(8,128)(2,1)S(1)}, u32[]{:S(2)}, u32[]{:S(2)}) collective-permute-start(bf16[64,1024]{1,0:T(8,128)(2,1)S(1)} %get-tuple-element.47), channel_id=1, source_target_pairs={{0,128},{16,144},{32,160},{48,176},{64,192},{80,208},{96,224},{112... | collective-permute-start | bytes 393224 | tf_op jit(solution)/shard_map/ppermute | solution.py:295
  37.9 23.6 %collective-permute-start.10 = (bf16[64,1024]{1,0:T(8,128)(2,1)S(1)}, bf16[64,1024]{1,0:T(8,128)(2,1)S(1)}, u32[]{:S(2)}, u32[]{:S(2)}) collective-permute-start(bf16[64,1024]{1,0:T(8,128)(2,1)S(1)} %get-tuple-element.48), channel_id=1, source_target_pairs={{0,144},{16,128},{32,176},{48,160},{64,208},{80,192},{96,240},{112... | collective-permute-start | bytes 393224 | tf_op jit(solution)/shard_map/ppermute | solution.py:295
  41.1 20.4 %collective-permute-start.11 = (bf16[64,1024]{1,0:T(8,128)(2,1)S(1)}, bf16[64,1024]{1,0:T(8,128)(2,1)S(1)}, u32[]{:S(2)}, u32[]{:S(2)}) collective-permute-start(bf16[64,1024]{1,0:T(8,128)(2,1)S(1)} %get-tuple-element.49), channel_id=1, source_target_pairs={{0,192},{16,208},{32,224},{48,240},{64,0},{80,16},{96,32},{112,48}... | collective-permute-start | bytes 393224 | tf_op jit(solution)/shard_map/ppermute | solution.py:295
  42.1 19.4 %collective-permute-start.12 = (bf16[64,1024]{1,0:T(8,128)(2,1)S(1)}, bf16[64,1024]{1,0:T(8,128)(2,1)S(1)}, u32[]{:S(2)}, u32[]{:S(2)}) collective-permute-start(bf16[64,1024]{1,0:T(8,128)(2,1)S(1)} %get-tuple-element.50), channel_id=1, source_target_pairs={{0,208},{16,192},{32,240},{48,224},{64,16},{80,0},{96,48},{112,32}... | collective-permute-start | bytes 393224 | tf_op jit(solution)/shard_map/ppermute | solution.py:295
  42.8 1.6 %copy-start.1 = (bf16[1024,1024]{1,0:T(8,128)(2,1)S(1)}, bf16[1024,1024]{1,0:T(8,128)(2,1)}, u32[]{:S(2)}) copy-start(bf16[1024,1024]{1,0:T(8,128)(2,1)} %wv_ref.5) | copy-start | bytes 6291460
  44.4 1.6 %copy-start.5 = (bf16[1024,1024]{1,0:T(8,128)(2,1)S(1)}, bf16[1024,1024]{1,0:T(8,128)(2,1)}, u32[]{:S(2)}) copy-start(bf16[1024,1024]{1,0:T(8,128)(2,1)} %wq_ref.1) | copy-start | bytes 6291460
  46.0 3.4 %copy-start.2 = (bf16[1024,1024]{1,0:T(8,128)(2,1)S(1)}, bf16[1024,1024]{1,0:T(8,128)(2,1)}, u32[]{:S(2)}) copy-start(bf16[1024,1024]{1,0:T(8,128)(2,1)} %wv_ref.5) | copy-start | bytes 6291460
  57.4 4.2 %copy-start.4 = (bf16[256,1024]{1,0:T(8,128)(2,1)S(1)}, bf16[256,1024]{1,0:T(8,128)(2,1)}, u32[]{:S(2)}) copy-start(bf16[256,1024]{1,0:T(8,128)(2,1)} %feat_ref.3) | copy-start | bytes 1572868
  57.4 4.2 %copy-start.6 = (bf16[1024,1024]{1,0:T(8,128)(2,1)S(1)}, bf16[1024,1024]{1,0:T(8,128)(2,1)}, u32[]{:S(2)}) copy-start(bf16[1024,1024]{1,0:T(8,128)(2,1)} %wo_ref.1) | copy-start | bytes 6291460
  57.4 4.2 %copy-start.7 = (s32[2,6]{1,0:T(2,128)S(1)}, s32[2,6]{1,0:T(2,128)}, u32[]{:S(2)}) copy-start(s32[2,6]{1,0:T(2,128)} %peers_ref.1) | copy-start | bytes 148
  57.4 4.2 %copy-start.9 = (s32[2]{0:T(128)S(1)}, s32[2]{0:T(128)}, u32[]{:S(2)}) copy-start(s32[2]{0:T(128)} %count_ref.1) | copy-start | bytes 28
where the time goes:
time: 75.4 us; the launch traced here: 75.3 us
  Pallas kernels  30.5 us (40%)
  starting transfers between devices  25.5 us (34%)
  waiting for transfers between devices  13.3 us (18%)
  local copies, waits for them, and re-layouts  5.11 us (7%)
  between operations  0.88 us (1%)
    pallas_call x6, Pallas kernels, run(): return pl.pallas_call(kernel, **kw)(*args)  30.5 us
    ppermute x6, starting transfers between devices, local(): lax.ppermute(relayed[i], 'grp', moved(i // 2, 0, i % 2))  9.27 us
    ppermute x1, waiting for transfers between devices, local(): across = lax.ppermute(a, 'grp', moved(0, 1, 0))  6.13 us
    ppermute x1, starting transfers between devices, local(): hi = lax.ppermute(down, 'rng', [(i, (i - 1) % ranks) for i in range(ranks)])  5.29 us
    unnamed x24, local copies, waits for them, and re-layouts  5.1 us
    ppermute x3, starting transfers between devices, local(): lax.ppermute(part, 'grp', moved(dx, 0, 0))  4.81 us
    ppermute x1, waiting for transfers between devices, local(): lo = lax.ppermute(up, 'rng', [(i, (i + 1) % ranks) for i in range(ranks)])  3.97 us
    ppermute x1, starting transfers between devices, local(): across = lax.ppermute(a, 'grp', moved(0, 1, 0))  3.82 us
  transfers between devices with their start and end apart: 13, of which 4 were waited for; matrix products, arithmetic and copies ran while one was open for 0% of the time, Pallas kernels for 21%

commit v1 on v0

v1 whole, which is shorter than its diff:
```python
import jax
import jax.numpy as jnp
from jax import lax
from jax.experimental import pallas as pl
from jax.experimental.pallas import tpu as pltpu
from jax.sharding import PartitionSpec as P


TILE = 128
PORTAL = 64
MAXLONG = 6
EPSILON = 1e-06
LANES = 128
HEAD = 64
CHUNK = 64
BLOCK = 256
PICKS = 8
SLOTS = 15
RIM = SLOTS * PORTAL
FIRST = (1, 2, 3, 4, 5, 6, 7, 8, 9, 12, 13)
SECOND = (10, 11, 14, 15)
MIB = 1024 * 1024
SCALE2 = HEAD**-0.5 * 1.4426950408889634
F32 = jnp.float32
NEVER = float(jnp.finfo(jnp.bfloat16).min)
BF16 = jnp.bfloat16

VMEM = pl.BlockSpec(memory_space=pltpu.VMEM)
SMEM = pl.BlockSpec(memory_space=pltpu.SMEM)
HBM = pl.BlockSpec(memory_space=pltpu.HBM)


def region(x, y, c):
    return (x % 4) * 4 + (y % 2) * 2 + c % 2


def moved(dx, dy, dc):
    return [
        (region(x, y, c), region(x + dx, y + dy, c ^ dc))
        for x in range(4)
        for y in range(2)
        for c in range(2)
    ]


def place_of(index):
    return index // 4, (index // 2) % 2, index % 2


def norm_kernel(feat_ref, a_ref, up_ref, down_ref):
    rows = feat_ref.shape[0]
    widened = feat_ref[...].astype(F32)
    factor = lax.rsqrt(jnp.mean(widened * widened, axis=1, keepdims=True) + EPSILON)
    normed = (widened * factor).astype(BF16)
    a_ref[...] = normed
    down_ref[...] = normed[:TILE]
    up_ref[...] = normed[rows - TILE :]


def pack_kernel(send_ref, a_ref, x1_ref, x2_ref, x3_ref, mate_ref, picks_ref):
    x, y, c = place_of(lax.axis_index("grp"))

    def pick(dx, dy, dc):
        return send_ref[0, ((x + dx) % 4) * 4 + (y ^ dy) * 2 + (c ^ dc)]

    def tile(index):
        return a_ref[pl.ds(pl.multiple_of(index * PORTAL, PORTAL), PORTAL)]

    for dx, ref in ((1, x1_ref), (2, x2_ref), (3, x3_ref)):
        for dc in range(2):
            ref[dc * PORTAL : (dc + 1) * PORTAL] = tile(pick(dx, 0, dc))
    mate_ref[...] = tile(pick(0, 0, 1))
    row = lax.broadcasted_iota(jnp.int32, picks_ref.shape, 0)
    picks = jnp.zeros(row.shape, jnp.int32)
    for i in range(PICKS):
        picks = jnp.where(row == i, pick(i // 2, 1, i % 2), picks)
    picks_ref[...] = picks.astype(F32).astype(BF16)


def relay_kernel(a_ref, picks_ref, *out_refs):
    rows = a_ref.shape[0]
    picks = picks_ref[...].astype(F32)
    for i, ref in enumerate(out_refs):
        pick = jnp.broadcast_to(picks[i : i + 1], (PORTAL, picks.shape[1]))
        tile = a_ref[:PORTAL].astype(F32)
        for k in range(1, rows // PORTAL):
            tile = jnp.where(
                pick == float(k), a_ref[k * PORTAL : (k + 1) * PORTAL].astype(F32), tile
            )
        ref[...] = tile.astype(BF16)


def dot(x, w):
    return jnp.dot(x, w, preferred_element_type=F32)


def block_cols(b):
    return slice(b * BLOCK, (b + 1) * BLOCK)


def low_lanes():
    return lax.broadcasted_iota(jnp.int32, (TILE, LANES), 1) < HEAD


def pair_queries(q):
    low = low_lanes()
    zero = jnp.zeros_like(q)
    return jnp.concatenate([jnp.where(low, q, zero), jnp.where(low, zero, q)], axis=0)


def unpair(x):
    return jnp.where(low_lanes(), x[:TILE], x[TILE:])


def set_eye(eye_ref):
    row = lax.broadcasted_iota(jnp.int32, eye_ref.shape, 0) % TILE
    lane = lax.broadcasted_iota(jnp.int32, eye_ref.shape, 1)
    eye_ref[...] = jnp.where(row == lane, 1.0, 0.0).astype(BF16)


def masked(keep):
    return jnp.where(keep, 0.0, NEVER).astype(BF16)


def pair_scores(q, eye, keys, mask):
    return lax.dot_general(
        jnp.concatenate([pair_queries(q), eye], axis=1),
        jnp.concatenate([keys, mask], axis=1),
        (((1,), (1,)), ((), ())),
        preferred_element_type=F32,
    )


def weigh(p, values):
    ones = jnp.ones(values.shape, BF16)
    both = dot(p, jnp.concatenate([values, ones], axis=1))
    return unpair(both[:, :LANES]), unpair(both[:, LANES:])


def chain(j, tiles):
    h, t = j // tiles, j % tiles
    return t, slice(t * TILE, (t + 1) * TILE), slice(h * LANES, (h + 1) * LANES)


def staged(count, fill, first, second, third):
    for j in range(count + 2):
        fill(j)
        if j < count:
            first(j)
        if 0 <= j - 1 < count:
            second(j - 1)
        if 0 <= j - 2:
            third(j - 2)


def spread_fill(parts, per_block):
    def fill(j):
        if j == 0:
            for part in parts:
                part(0)
        b, i = j // per_block + 1, j % per_block
        if i < len(parts):
            parts[i](b)

    return fill


def here_kernel(
    reach_ref, a_ref, wq_ref, wk_ref, wv_ref, q_ref, acc_ref, max_ref, sum_ref,
    k_s, v_s, eye_s, mask_s, s0, s1, p0, p1,
):
    rows, width = q_ref.shape
    tiles = rows // TILE
    blocks = width // BLOCK
    s_s, p_s = (s0, s1), (p0, p1)
    set_eye(eye_s)
    key = lax.broadcasted_iota(jnp.int32, (rows, LANES), 0)
    place = lax.broadcasted_iota(jnp.int32, (rows, LANES), 1)
    for t in range(tiles):
        mask_s[t * rows : (t + 1) * rows] = masked(jnp.abs(place + t * TILE - key) <= reach_ref[0])

    def project(w_ref, out_ref, scale=None):
        def part(b):
            if b < blocks:
                cols = block_cols(b)
                product = dot(a_ref[:rows], w_ref[:, cols])
                if scale is not None:
                    product = product * scale
                out_ref[:, cols] = product.astype(BF16)

        return part

    def first(j):
        t, here, cols = chain(j, tiles)
        mask = mask_s[t * rows : (t + 1) * rows]
        s_s[j % 2][...] = pair_scores(q_ref[here, cols], eye_s[...], k_s[:, cols], mask)

    def second(j):
        for r in range(0, 2 * TILE, CHUNK):
            s = s_s[j % 2][r : r + CHUNK]
            m = jnp.max(s, axis=1, keepdims=True)
            max_ref[j, r : r + CHUNK] = jnp.broadcast_to(m, (CHUNK, LANES))
            p_s[j % 2][r : r + CHUNK] = jnp.exp2(s - m).astype(BF16)

    def third(j):
        _, here, cols = chain(j, tiles)
        acc, total = weigh(p_s[j % 2][...], v_s[:, cols])
        acc_ref[here, cols] = acc
        sum_ref[here, cols] = total

    fill = spread_fill(
        [project(wq_ref, q_ref, SCALE2), project(wk_ref, k_s), project(wv_ref, v_s)],
        tiles * BLOCK // LANES,
    )
    staged(tiles * width // LANES, fill, first, second, third)


def tile_rows(pos):
    return slice((pos - 1) * PORTAL, pos * PORTAL)


def far_kernel(
    mine_ref, l1_ref, l4_ref, l5_ref, x1_ref, x2_ref, x3_ref, swap_ref, lo_ref, hi_ref,
    wk_ref, wv_ref, ke_ref, ve_ref, x_s,
):
    tiles = {8: mine_ref[...], 9: l1_ref[...], 12: l4_ref[...], 13: l5_ref[...]}
    for dx, ref in ((1, x1_ref), (2, x2_ref), (3, x3_ref)):
        tiles[2 * dx] = ref[:PORTAL]
    for i, pos in enumerate((1, 3, 5, 7)):
        tiles[pos] = swap_ref[i * PORTAL : (i + 1) * PORTAL]
    for i, pos in enumerate(FIRST):
        x_s[tile_rows(i + 1)] = tiles[pos]
    near = len(FIRST) * PORTAL
    x_s[near : near + TILE] = lo_ref[...]
    x_s[near + TILE :] = hi_ref[...]
    for b in range(wk_ref.shape[1] // BLOCK):
        cols = block_cols(b)
        for w_ref, out_ref in ((wk_ref, ke_ref), (wv_ref, ve_ref)):
            product = dot(x_s[...], w_ref[:, cols]).astype(BF16)
            for i, pos in enumerate(FIRST):
                out_ref[tile_rows(pos), cols] = product[tile_rows(i + 1)]
            out_ref[RIM:, cols] = product[near:]


def last_kernel(
    peers_hbm, count_hbm, reach_ref, q_ref, acc_ref, max_ref, sum_ref, feat_ref, ke_ref, ve_ref,
    l0, l1, l2, l3, wk_ref, wv_ref, wo_ref, out_hbm, k_ref, v_ref,
    x_s, att_s, kl_s, vl_s, eye_s, mask_s, keep0, keep1, s0, s1, p0, p1, out_s,
    peers_ref, count_ref, sems,
):
    rows, width = q_ref.shape
    tiles = rows // TILE
    blocks = width // BLOCK
    span = MAXLONG * PORTAL
    keys = span + TILE
    s_s, p_s, keep_s = (s0, s1), (p0, p1), (keep0, keep1)
    peers_copy = pltpu.make_async_copy(peers_hbm, peers_ref, sems.at[0])
    count_copy = pltpu.make_async_copy(count_hbm, count_ref, sems.at[1])
    peers_copy.start()
    count_copy.start()
    for i, ref in enumerate((l0, l1, l2, l3)):
        x_s[i * PORTAL : (i + 1) * PORTAL] = ref[...]
    x, y, c = place_of(lax.axis_index("grp"))
    set_eye(eye_s)
    near = lax.broadcasted_iota(jnp.int32, (TILE, LANES), 0)
    place = lax.broadcasted_iota(jnp.int32, (TILE, LANES), 1)
    slot = lax.broadcasted_iota(jnp.int32, (span, LANES), 0) // PORTAL
    for t in range(tiles):
        gap = place + TILE - near if t == 0 else near + TILE - place
        mask_s[t * keys + span : (t + 1) * keys] = masked(gap <= reach_ref[0])
    starts = []

    def lists():
        peers_copy.wait()
        count_copy.wait()
        for t in range(tiles):
            mask_s[t * keys : t * keys + span] = masked(slot < count_ref[t])
            for s in range(MAXLONG):
                px, py, pc = place_of(peers_ref[t, s])
                pos = (y ^ py) * 8 + ((x - px + 4) % 4) * 2 + (c ^ pc)
                starts.append(pl.multiple_of((pos - 1) * PORTAL, PORTAL))

    def project(w_ref, all_ref, listed_ref):
        def part(b):
            if b < blocks:
                cols = block_cols(b)
                product = dot(x_s[...], w_ref[:, cols]).astype(BF16)
                for i, pos in enumerate(SECOND):
                    all_ref[tile_rows(pos), cols] = product[tile_rows(i + 1)]
                if not starts:
                    lists()
                for t in range(tiles):
                    for s in range(MAXLONG):
                        row = t * keys + s * PORTAL
                        listed_ref[row : row + PORTAL, cols] = all_ref[
                            pl.ds(starts[t * MAXLONG + s], PORTAL), cols
                        ]
                    rim = RIM + t * TILE
                    listed_ref[t * keys + span : (t + 1) * keys, cols] = all_ref[
                        rim : rim + TILE, cols
                    ]

        return part

    def first(j):
        t, here, cols = chain(j, tiles)
        mine = slice(t * keys, (t + 1) * keys)
        s_s[j % 2][...] = pair_scores(q_ref[here, cols], eye_s[...], kl_s[mine, cols], mask_s[mine])

    def second(j):
        for r in range(0, 2 * TILE, CHUNK):
            s = s_s[j % 2][r : r + CHUNK]
            band_max = max_ref[j, r : r + CHUNK]
            m = jnp.maximum(jnp.max(s, axis=1, keepdims=True), band_max)
            keep_s[j % 2][r : r + CHUNK] = jnp.exp2(band_max - m)
            p = jnp.exp2(s - jnp.concatenate([m] * (keys // LANES), axis=1))
            p_s[j % 2][r : r + CHUNK] = p.astype(BF16)

    def third(j):
        t, here, cols = chain(j, tiles)
        acc, total = weigh(p_s[j % 2][...], vl_s[t * keys : (t + 1) * keys, cols])
        keep = unpair(keep_s[j % 2][...])
        acc = acc + keep * acc_ref[here, cols]
        total = total + keep * sum_ref[here, cols]
        att_s[here, cols] = (acc / total).astype(BF16)

    fill = spread_fill(
        [project(wk_ref, k_ref, kl_s), project(wv_ref, v_ref, vl_s)], tiles * BLOCK // LANES
    )
    staged(tiles * width // LANES, fill, first, second, third)
    copies = []
    for b in range(blocks):
        cols = block_cols(b)
        projected = dot(att_s[...], wo_ref[:, cols])
        out_s[:, cols] = (feat_ref[:, cols].astype(F32) + projected).astype(BF16)
        copies.append(
            pltpu.make_async_copy(out_s.at[:, cols], out_hbm.at[:, cols], sems.at[2 + b])
        )
        copies[-1].start()
    for copy in copies:
        copy.wait()


def named(kernel, **kw):
    def run(*args):
        return pl.pallas_call(kernel, **kw)(*args)

    return run


def shape(*dims, dtype=BF16):
    return jax.ShapeDtypeStruct(dims, dtype)


def params(mib):
    return pltpu.CompilerParams(vmem_limit_bytes=mib * MIB)


def local(
    features, query_weight, key_weight, value_weight, out_weight,
    band_reach, long_peers, long_count, send_tile,
):
    rows, width = features.shape
    ranks = lax.axis_size("rng")
    tall = shape(2 * PORTAL, width)
    half = shape(TILE, width)
    tile = shape(PORTAL, width)
    square = shape(rows, width)
    a, up, down = named(
        norm_kernel,
        out_shape=(square, half, half),
        in_specs=[VMEM],
        out_specs=(VMEM,) * 3,
        compiler_params=params(4),
    )(features)
    across = lax.ppermute(a, "grp", moved(0, 1, 0))
    x1, x2, x3, mate, picks = named(
        pack_kernel,
        out_shape=(tall, tall, tall, tile, shape(PICKS, width)),
        in_specs=[SMEM, VMEM],
        out_specs=(VMEM,) * 5,
        cost_estimate=pl.CostEstimate(flops=10**10, bytes_accessed=2**23, transcendentals=0),
        compiler_params=params(4),
    )(send_tile, a)
    x1, x2, x3 = [
        lax.ppermute(part, "grp", moved(dx, 0, 0))
        for dx, part in ((1, x1), (2, x2), (3, x3))
    ]
    picks = lax.ppermute(picks, "grp", moved(0, 1, 0))
    wide = shape(rows, width, dtype=F32)
    chains = rows // TILE * width // LANES
    tops = shape(chains, 2 * TILE, LANES, dtype=F32)

    def stages(keys):
        return [pltpu.VMEM((2 * TILE, keys), F32)] * 2 + [pltpu.VMEM((2 * TILE, keys), BF16)] * 2

    queries, acc, top, total = named(
        here_kernel,
        out_shape=(square, wide, tops, wide),
        in_specs=[SMEM] + [VMEM] * 4,
        out_specs=(VMEM,) * 4,
        scratch_shapes=[pltpu.VMEM((rows, width), BF16)] * 2
        + [pltpu.VMEM((2 * TILE, LANES), BF16), pltpu.VMEM((rows // TILE * rows, LANES), BF16)]
        + stages(rows),
        compiler_params=params(8),
    )(band_reach, a, query_weight, key_weight, value_weight)
    up, down, queries, x1, x3 = lax.optimization_barrier((up, down, queries, x1, x3))
    lo = lax.ppermute(up, "rng", [(i, (i + 1) % ranks) for i in range(ranks)])
    hi = lax.ppermute(down, "rng", [(i, (i - 1) % ranks) for i in range(ranks)])
    relayed = named(
        relay_kernel,
        out_shape=(tile,) * PICKS,
        in_specs=[VMEM] * 2,
        out_specs=(VMEM,) * PICKS,
        compiler_params=params(4),
    )(across, picks)
    late = {i: lax.ppermute(relayed[i], "grp", moved(i // 2, 0, i % 2)) for i in range(1, PICKS)}
    swapped = lax.ppermute(
        jnp.concatenate([mate, x1[PORTAL:], x2[PORTAL:], x3[PORTAL:]], axis=0),
        "grp",
        moved(0, 0, 1),
    )
    far = shape(RIM + 2 * TILE, width)
    far_rows = len(FIRST) * PORTAL + 2 * TILE
    far_keys, far_values = named(
        far_kernel,
        out_shape=(far, far),
        in_specs=[VMEM] * 12,
        out_specs=(VMEM,) * 2,
        scratch_shapes=[pltpu.VMEM((far_rows, width), BF16)],
        compiler_params=params(8),
    )(
        relayed[0], late[1], late[4], late[5], x1, x2, x3, swapped, lo, hi,
        key_weight, value_weight,
    )
    span = MAXLONG * PORTAL + TILE
    listed = rows // TILE * span
    updated, _, _ = named(
        last_kernel,
        out_shape=(square, far, far),
        in_specs=[HBM, HBM, SMEM] + [VMEM] * (7 + len(SECOND) + 3),
        out_specs=(HBM, VMEM, VMEM),
        scratch_shapes=[
            pltpu.VMEM((len(SECOND) * PORTAL, width), BF16),
            pltpu.VMEM((rows, width), BF16),
            pltpu.VMEM((listed, width), BF16),
            pltpu.VMEM((listed, width), BF16),
            pltpu.VMEM((2 * TILE, LANES), BF16),
            pltpu.VMEM((listed, LANES), BF16),
            pltpu.VMEM((2 * TILE, LANES), F32),
            pltpu.VMEM((2 * TILE, LANES), F32),
        ]
        + stages(span)
        + [
            pltpu.VMEM((rows, width), BF16),
            pltpu.SMEM(long_peers.shape, jnp.int32),
            pltpu.SMEM(long_count.shape, jnp.int32),
            pltpu.SemaphoreType.DMA((2 + width // BLOCK,)),
        ],
        input_output_aliases={8: 1, 9: 2},
        compiler_params=params(14),
    )(
        long_peers, long_count, band_reach, queries, acc, top, total, features,
        far_keys, far_values, late[2], late[3], late[6], late[7], key_weight, value_weight, out_weight,
    )
    return updated


def solution(mesh):
    spread = ("grp", "rng")
    return jax.shard_map(
        local,
        mesh=mesh,
        in_specs=(
            P(spread, None), P(), P(), P(), P(),
            P(spread), P(spread, None), P(spread), P(spread, None),
        ),
        out_specs=P(spread, None),
        check_vma=False,
    )
```

time: 75.4 us -> 60.3 us (0.80)
  Pallas kernels: 30.5 us -> 15.3 us
  local copies, waits for them, and re-layouts: 5.11 us -> 1.75 us
  starting transfers between devices: 25.5 us -> 27.4 us
  waiting for transfers between devices: 13.3 us -> 14.5 us
    pallas_call x6, Pallas kernels: 30.5 us -> 15.3 us  [run(): return pl.pallas_call(kernel, **kw)(*args)]
    ppermute x1 -> x2, waiting for transfers between devices: 0.01 us -> 6.69 us  [the longest x1 6.69 us: local(): picks = lax.ppermute(picks, 'grp', moved(0, 1, 0))]
    ppermute x1, waiting for transfers between devices: 6.13 us -> 0.01 us  [local(): across = lax.ppermute(a, 'grp', moved(0, 1, 0))]
    ppermute x6 -> x7, waiting for transfers between devices: 0.02 us -> 4.03 us  [local(): lax.ppermute(relayed[i], 'grp', moved(i // 2, 0, i % 2))]
    ppermute x1, waiting for transfers between devices: 3.97 us -> 0.01 us  [local(): lo = lax.ppermute(up, 'rng', [(i, (i + 1) % ranks) for i in range(ranks)])]
    unnamed x24 -> x18, local copies, waits for them, and re-layouts: 5.1 us -> 1.72 us
    ppermute x1 -> x2, starting transfers between devices: 1.9 us -> 4.24 us  [the longest x1 2.62 us: local(): picks = lax.ppermute(picks, 'grp', moved(0, 1, 0))]
    ppermute x1, starting transfers between devices: 3.82 us -> 2.91 us  [local(): across = lax.ppermute(a, 'grp', moved(0, 1, 0))]
  transfers between devices with their start and end apart: 13 -> 15, of which waited for: 4 -> 4; matrix products, arithmetic and copies ran while one was open for 0% -> 0% of each run, Pallas kernels for 21% -> 14%
where the time goes in v1:
time: 60.3 us; the launch traced here: 60.1 us
  starting transfers between devices  27.4 us (45%)
  Pallas kernels  15.3 us (25%)
  waiting for transfers between devices  14.5 us (24%)
  local copies, waits for them, and re-layouts  1.75 us (3%)
  between operations  1.01 us (2%)
    pallas_call x6, Pallas kernels, run(): return pl.pallas_call(kernel, **kw)(*args)  15.3 us
    ppermute x7, starting transfers between devices, local(): lax.ppermute(relayed[i], 'grp', moved(i // 2, 0, i % 2))  8.59 us
    ppermute x1, waiting for transfers between devices, local(): picks = lax.ppermute(picks, 'grp', moved(0, 1, 0))  6.69 us
    ppermute x1, starting transfers between devices, local(): hi = lax.ppermute(down, 'rng', [(i, (i - 1) % ranks) for i in range(ranks)])  5.29 us
    ppermute x3, starting transfers between devices, local(): lax.ppermute(part, 'grp', moved(dx, 0, 0))  5.1 us
    ppermute x7, waiting for transfers between devices, local(): lax.ppermute(relayed[i], 'grp', moved(i // 2, 0, i % 2))  4.03 us
    ppermute x3, waiting for transfers between devices, local(): lax.ppermute(part, 'grp', moved(dx, 0, 0))  3.82 us
    ppermute x1, starting transfers between devices, local(): across = lax.ppermute(a, 'grp', moved(0, 1, 0))  2.91 us
  transfers between devices with their start and end apart: 15, of which 4 were waited for; matrix products, arithmetic and copies ran while one was open for 0% of the time, Pallas kernels for 14%

profile of v1, /device:TPU:1, one launch (start us, length us, event | category | flops | bytes accessed | tf_op | source)
XLA Modules:
  0.0 60.1 jit_solution(15001534149528564618)
XLA Ops:
  0.0 1.0 %copy-done.3 = bf16[256,1024]{1,0:T(8,128)(2,1)S(1)} copy-done((bf16[256,1024]{1,0:T(8,128)(2,1)S(1)}, bf16[256,1024]{1,0:T(8,128)(2,1)}, u32[]{:S(2)}) %copy-start.3) | copy-done | bytes 524312
  1.0 0.2 shard_map.91
  1.2 0.0 copy-start.8
  1.3 0.6 %copy-done.8 = s32[1,16]{1,0:T(1,128)S(1)} copy-done((s32[1,16]{1,0:T(1,128)S(1)}, s32[1,16]{1,0:T(1,128)}, u32[]{:S(2)}) %copy-start.8) | copy-done | bytes 88
  1.9 0.6 %shard_map.93 = (bf16[128,1024]{1,0:T(8,128)(2,1)S(1)}, bf16[128,1024]{1,0:T(8,128)(2,1)S(1)}, bf16[128,1024]{1,0:T(8,128)(2,1)S(1)}, bf16[64,1024]{1,0:T(8,128)(2,1)S(1)}, bf16[8,1024]{1,0:T(8,128)(2,1)S(1)}) custom-call(s32[1,16]{1,0:T(1,128)S(1)} %copy-done.8, bf16[256,1024]{1,0:T(8,128)(2,1)S(1)} %get-tuple-element.35.a_ref), custom_call_target="tpu_custom_call" | custom-call | flops 10000000000 | bytes 8388608 | tf_op jit(solution)/shard_map/pallas_call | solution.py:346
  2.5 2.1 %collective-permute-start = (bf16[128,1024]{1,0:T(8,128)(2,1)S(1)}, bf16[128,1024]{1,0:T(8,128)(2,1)S(1)}, u32[]{:S(2)}, u32[]{:S(2)}) collective-permute-start(bf16[128,1024]{1,0:T(8,128)(2,1)S(1)} %get-tuple-element.37), channel_id=1, source_target_pairs={{0,64},{16,80},{32,96},{48,112},{64,128},{80,144},{96,160},{112,17... | collective-permute-start | bytes 786440 | tf_op jit(solution)/shard_map/ppermute | solution.py:386
  4.6 1.4 %collective-permute-start.1 = (bf16[128,1024]{1,0:T(8,128)(2,1)S(1)}, bf16[128,1024]{1,0:T(8,128)(2,1)S(1)}, u32[]{:S(2)}, u32[]{:S(2)}) collective-permute-start(bf16[128,1024]{1,0:T(8,128)(2,1)S(1)} %get-tuple-element.38), channel_id=1, source_target_pairs={{0,192},{16,208},{32,224},{48,240},{64,0},{80,16},{96,32},{112,48}... | collective-permute-start | bytes 786440 | tf_op jit(solution)/shard_map/ppermute | solution.py:386
  6.0 1.6 %collective-permute-start.7 = (bf16[128,1024]{1,0:T(8,128)(2,1)S(1)}, bf16[128,1024]{1,0:T(8,128)(2,1)S(1)}, u32[]{:S(2)}, u32[]{:S(2)}) collective-permute-start(bf16[128,1024]{1,0:T(8,128)(2,1)S(1)} %get-tuple-element.49), channel_id=1, source_target_pairs={{0,128},{16,144},{32,160},{48,176},{64,192},{80,208},{96,224},{112... | collective-permute-start | bytes 786440 | tf_op jit(solution)/shard_map/ppermute | solution.py:386
  7.6 2.9 %collective-permute-start.2 = (bf16[256,1024]{1,0:T(8,128)(2,1)S(1)}, bf16[256,1024]{1,0:T(8,128)(2,1)S(1)}, u32[]{:S(2)}, u32[]{:S(2)}) collective-permute-start(bf16[256,1024]{1,0:T(8,128)(2,1)S(1)} %get-tuple-element.35.a_ref), channel_id=1, source_target_pairs={{0,32},{16,48},{32,0},{48,16},{64,96},{80,112},{96,64},{112,80},{1... | collective-permute-start | bytes 1572872 | tf_op jit(solution)/shard_map/ppermute | solution.py:376
  11.2 3.3 %shard_map.92 = (bf16[256,1024]{1,0:T(8,128)(2,1)S(1)}, f32[256,1024]{1,0:T(8,128)S(1)}, f32[16,256,128]{2,1,0:T(8,128)S(1)}, f32[256,1024]{1,0:T(8,128)S(1)}) custom-call(s32[1]{0:T(128)S(6)} %copy.14.reach_ref, bf16[256,1024]{1,0:T(8,128)(2,1)S(1)} %get-tuple-element.35.a_ref, bf16[1024,1024]{1,0:T(8,128)(2,1)S(1)} %copy-done.5, ...), custom_call_target="tpu_custom_call" | custom-call | tf_op jit(solution)/shard_map/pallas_call | solution.py:346
  14.6 0.0 collective-permute-done.1.x3_ref
  14.6 3.8 %collective-permute-done.7.x2_ref = bf16[128,1024]{1,0:T(8,128)(2,1)S(1)} collective-permute-done((bf16[128,1024]{1,0:T(8,128)(2,1)S(1)}, bf16[128,1024]{1,0:T(8,128)(2,1)S(1)}, u32[]{:S(2)}, u32[]{:S(2)}) %collective-permute-start.7) | collective-permute-done | bytes 262176 | tf_op jit(solution)/shard_map/ppermute | solution.py:386
  18.5 1.6 %collective-permute-start.8 = (bf16[256,1024]{1,0:T(8,128)(2,1)S(1)}, bf16[256,1024]{1,0:T(8,128)(2,1)S(1)}, u32[]{:S(2)}, u32[]{:S(2)}) collective-permute-start(bf16[256,1024]{1,0:T(8,128)(2,1)S(1)} %pad_maximum_fusion), channel_id=1, source_target_pairs={{0,16},{16,0},{32,48},{48,32},{64,80},{80,64},{96,112},{112,96},{1... | collective-permute-start | bytes 1572872 | tf_op jit(solution)/shard_map/ppermute | solution.py:418
  20.1 1.3 %collective-permute-start.9 = (bf16[128,1024]{1,0:T(8,128)(2,1)S(1)}, bf16[128,1024]{1,0:T(8,128)(2,1)S(1)}, u32[]{:S(2)}, u32[]{:S(2)}) collective-permute-start(bf16[128,1024]{1,0:T(8,128)(2,1)S(1)} %get-tuple-element.52), channel_id=1, source_target_pairs={{0,1},{1,2},{2,3},{3,4},{4,5},{5,6},{6,7},{7,8},{8,9},{9,10},{10,1... | collective-permute-start | bytes 786440 | tf_op jit(solution)/shard_map/ppermute | solution.py:408
  21.4 5.3 %collective-permute-start.10 = (bf16[128,1024]{1,0:T(8,128)(2,1)S(1)}, bf16[128,1024]{1,0:T(8,128)(2,1)S(1)}, u32[]{:S(2)}, u32[]{:S(2)}) collective-permute-start(bf16[128,1024]{1,0:T(8,128)(2,1)S(1)} %get-tuple-element.53), channel_id=1, source_target_pairs={{0,15},{1,0},{2,1},{3,2},{4,3},{5,4},{6,5},{7,6},{8,7},{9,8},{10,9... | collective-permute-start | bytes 786440 | tf_op jit(solution)/shard_map/ppermute | solution.py:409
  26.7 2.6 %collective-permute-start.3 = (bf16[8,1024]{1,0:T(8,128)(2,1)S(1)}, bf16[8,1024]{1,0:T(8,128)(2,1)S(1)}, u32[]{:S(2)}, u32[]{:S(2)}) collective-permute-start(bf16[8,1024]{1,0:T(8,128)(2,1)S(1)} %get-tuple-element.43), channel_id=1, source_target_pairs={{0,32},{16,48},{32,0},{48,16},{64,96},{80,112},{96,64},{112,80},{1... | collective-permute-start | bytes 49160 | tf_op jit(solution)/shard_map/ppermute | solution.py:389
  29.3 6.7 %collective-permute-done.3.picks_ref = bf16[8,1024]{1,0:T(8,128)(2,1)S(1)} collective-permute-done((bf16[8,1024]{1,0:T(8,128)(2,1)S(1)}, bf16[8,1024]{1,0:T(8,128)(2,1)S(1)}, u32[]{:S(2)}, u32[]{:S(2)}) %collective-permute-start.3) | collective-permute-done | bytes 16416 | tf_op jit(solution)/shard_map/ppermute | solution.py:389
  36.0 0.6 %shard_map.94 = (bf16[64,1024]{1,0:T(8,128)(2,1)S(1)}, bf16[64,1024]{1,0:T(8,128)(2,1)S(1)}, bf16[64,1024]{1,0:T(8,128)(2,1)S(1)}, bf16[64,1024]{1,0:T(8,128)(2,...) custom-call(bf16[256,1024]{1,0:T(8,128)(2,1)S(1)} %collective-permut, ...), custom_call_target="tpu_custom_call" | custom-call | tf_op jit(solution)/shard_map/pallas_call | solution.py:346
  36.7 1.3 %collective-permute-start.4 = (bf16[64,1024]{1,0:T(8,128)(2,1)S(1)}, bf16[64,1024]{1,0:T(8,128)(2,1)S(1)}, u32[]{:S(2)}, u32[]{:S(2)}) collective-permute-start(bf16[64,1024]{1,0:T(8,128)(2,1)S(1)} %get-tuple-element.45), channel_id=1, source_target_pairs={{0,16},{16,0},{32,48},{48,32},{64,80},{80,64},{96,112},{112,96},{1... | collective-permute-start | bytes 393224 | tf_op jit(solution)/shard_map/ppermute | solution.py:417
  38.0 0.5 collective-permute-start.5
  38.5 2.7 %collective-permute-start.6 = (bf16[64,1024]{1,0:T(8,128)(2,1)S(1)}, bf16[64,1024]{1,0:T(8,128)(2,1)S(1)}, u32[]{:S(2)}, u32[]{:S(2)}) collective-permute-start(bf16[64,1024]{1,0:T(8,128)(2,1)S(1)} %get-tuple-element.47), channel_id=1, source_target_pairs={{0,144},{16,128},{32,176},{48,160},{64,208},{80,192},{96,240},{112... | collective-permute-start | bytes 393224 | tf_op jit(solution)/shard_map/ppermute | solution.py:417
  41.2 0.0 collective-permute-done.10.hi_ref
  41.2 0.9 %collective-permute-start.11 = (bf16[64,1024]{1,0:T(8,128)(2,1)S(1)}, bf16[64,1024]{1,0:T(8,128)(2,1)S(1)}, u32[]{:S(2)}, u32[]{:S(2)}) collective-permute-start(bf16[64,1024]{1,0:T(8,128)(2,1)S(1)} %get-tuple-element.56), channel_id=1, source_target_pairs={{0,64},{16,80},{32,96},{48,112},{64,128},{80,144},{96,160},{112,17... | collective-permute-start | bytes 393224 | tf_op jit(solution)/shard_map/ppermute | solution.py:417
  42.1 0.0 collective-permute-done.4.l1_ref
  42.1 0.3 collective-permute-start.12
  42.4 2.1 %collective-permute-done.5.l4_ref = bf16[64,1024]{1,0:T(8,128)(2,1)S(1)} collective-permute-done((bf16[64,1024]{1,0:T(8,128)(2,1)S(1)}, bf16[64,1024]{1,0:T(8,128)(2,1)S(1)}, u32[]{:S(2)}, u32[]{:S(2)}) %collective-permute-start.5) | collective-permute-done | bytes 131104 | tf_op jit(solution)/shard_map/ppermute | solution.py:417
  44.4 1.7 %collective-permute-start.13 = (bf16[64,1024]{1,0:T(8,128)(2,1)S(1)}, bf16[64,1024]{1,0:T(8,128)(2,1)S(1)}, u32[]{:S(2)}, u32[]{:S(2)}) collective-permute-start(bf16[64,1024]{1,0:T(8,128)(2,1)S(1)} %get-tuple-element.58), channel_id=1, source_target_pairs={{0,192},{16,208},{32,224},{48,240},{64,0},{80,16},{96,32},{112,48}... | collective-permute-start | bytes 393224 | tf_op jit(solution)/shard_map/ppermute | solution.py:417
  46.2 1.9 %collective-permute-done.6.l5_ref = bf16[64,1024]{1,0:T(8,128)(2,1)S(1)} collective-permute-done((bf16[64,1024]{1,0:T(8,128)(2,1)S(1)}, bf16[64,1024]{1,0:T(8,128)(2,1)S(1)}, u32[]{:S(2)}, u32[]{:S(2)}) %collective-permute-start.6) | collective-permute-done | bytes 131104 | tf_op jit(solution)/shard_map/ppermute | solution.py:417
  48.1 1.1 %collective-permute-start.14 = (bf16[64,1024]{1,0:T(8,128)(2,1)S(1)}, bf16[64,1024]{1,0:T(8,128)(2,1)S(1)}, u32[]{:S(2)}, u32[]{:S(2)}) collective-permute-start(bf16[64,1024]{1,0:T(8,128)(2,1)S(1)} %get-tuple-element.59), channel_id=1, source_target_pairs={{0,208},{16,192},{32,240},{48,224},{64,16},{80,0},{96,48},{112,32}... | collective-permute-start | bytes 393224 | tf_op jit(solution)/shard_map/ppermute | solution.py:417
  49.3 0.0 copy-start.7
  49.3 4.3 %shard_map.95 = (bf16[1216,1024]{1,0:T(8,128)(2,1)S(1)}, bf16[1216,1024]{1,0:T(8,128)(2,1)S(1)}) custom-call(bf16[64,1024]{1,0:T(8,128)(2,1)S(1)} %get-tuple-element.44.mine_ref, bf16[64,1024]{1,0:T(8,128)(2,1)S(1)} %collective-permute-done.4.l1_ref, bf16[64,1024]{1,0:T(8,128)(2,1)S(1)} %collective-permute-done.5.l4_ref, ...), custom_call_target="tpu_custom_call" | custom-call | tf_op jit(solution)/shard_map/pallas_call | solution.py:346
  53.6 6.3 %shard_map.96 = (bf16[256,1024]{1,0:T(8,128)(2,1)}, bf16[1216,1024]{1,0:T(8,128)(2,1)S(1)}, bf16[1216,1024]{1,0:T(8,128)(2,1)S(1)}) custom-call(s32[2,6]{1,0:T(2,128)S(1)} %copy-done.6, s32[2]{0:T(128)S(1)} %copy-done.7, s32[1]{0:T(128)S(6)} %copy.14.reach_ref, ...), custom_call_target="tpu_custom_call", output_to_operand_aliasing={{1}: (8, {}), {2}: (9, {})} | custom-call | tf_op jit(solution)/shard_map/pallas_call | solution.py:346
  (26 shorter events, 0.1 us)
Async XLA Ops:
  0.0 1.0 %copy-start.3 = (bf16[256,1024]{1,0:T(8,128)(2,1)S(1)}, bf16[256,1024]{1,0:T(8,128)(2,1)}, u32[]{:S(2)}) copy-start(bf16[256,1024]{1,0:T(8,128)(2,1)} %feat_ref.3) | copy-start | bytes 1572868
  1.2 0.7 %copy-start.8 = (s32[1,16]{1,0:T(1,128)S(1)}, s32[1,16]{1,0:T(1,128)}, u32[]{:S(2)}) copy-start(s32[1,16]{1,0:T(1,128)} %send_ref.1) | copy-start | bytes 196
  1.9 9.3 %copy-start = (bf16[1024,1024]{1,0:T(8,128)(2,1)S(1)}, bf16[1024,1024]{1,0:T(8,128)(2,1)}, u32[]{:S(2)}) copy-start(bf16[1024,1024]{1,0:T(8,128)(2,1)} %wk_ref.5) | copy-start | bytes 6291460
  1.9 9.3 %copy-start.1 = (bf16[1024,1024]{1,0:T(8,128)(2,1)S(1)}, bf16[1024,1024]{1,0:T(8,128)(2,1)}, u32[]{:S(2)}) copy-start(bf16[1024,1024]{1,0:T(8,128)(2,1)} %wv_ref.5) | copy-start | bytes 6291460
  1.9 9.3 %copy-start.5 = (bf16[1024,1024]{1,0:T(8,128)(2,1)S(1)}, bf16[1024,1024]{1,0:T(8,128)(2,1)}, u32[]{:S(2)}) copy-start(bf16[1024,1024]{1,0:T(8,128)(2,1)} %wq_ref.1) | copy-start | bytes 6291460
  2.5 12.0 %collective-permute-start = (bf16[128,1024]{1,0:T(8,128)(2,1)S(1)}, bf16[128,1024]{1,0:T(8,128)(2,1)S(1)}, u32[]{:S(2)}, u32[]{:S(2)}) collective-permute-start(bf16[128,1024]{1,0:T(8,128)(2,1)S(1)} %get-tuple-element.37), channel_id=1, source_target_pairs={{0,64},{16,80},{32,96},{48,112},{64,128},{80,144},{96,160},{112,17... | collective-permute-start | bytes 786440 | tf_op jit(solution)/shard_map/ppermute | solution.py:386
  4.6 9.9 %collective-permute-start.1 = (bf16[128,1024]{1,0:T(8,128)(2,1)S(1)}, bf16[128,1024]{1,0:T(8,128)(2,1)S(1)}, u32[]{:S(2)}, u32[]{:S(2)}) collective-permute-start(bf16[128,1024]{1,0:T(8,128)(2,1)S(1)} %get-tuple-element.38), channel_id=1, source_target_pairs={{0,192},{16,208},{32,224},{48,240},{64,0},{80,16},{96,32},{112,48}... | collective-permute-start | bytes 786440 | tf_op jit(solution)/shard_map/ppermute | solution.py:386
  6.0 12.4 %collective-permute-start.7 = (bf16[128,1024]{1,0:T(8,128)(2,1)S(1)}, bf16[128,1024]{1,0:T(8,128)(2,1)S(1)}, u32[]{:S(2)}, u32[]{:S(2)}) collective-permute-start(bf16[128,1024]{1,0:T(8,128)(2,1)S(1)} %get-tuple-element.49), channel_id=1, source_target_pairs={{0,128},{16,144},{32,160},{48,176},{64,192},{80,208},{96,224},{112... | collective-permute-start | bytes 786440 | tf_op jit(solution)/shard_map/ppermute | solution.py:386
  7.6 28.4 %collective-permute-start.2 = (bf16[256,1024]{1,0:T(8,128)(2,1)S(1)}, bf16[256,1024]{1,0:T(8,128)(2,1)S(1)}, u32[]{:S(2)}, u32[]{:S(2)}) collective-permute-start(bf16[256,1024]{1,0:T(8,128)(2,1)S(1)} %get-tuple-element.35.a_ref), channel_id=1, source_target_pairs={{0,32},{16,48},{32,0},{48,16},{64,96},{80,112},{96,64},{112,80},{1... | collective-permute-start | bytes 1572872 | tf_op jit(solution)/shard_map/ppermute | solution.py:376
  18.5 30.8 %collective-permute-start.8 = (bf16[256,1024]{1,0:T(8,128)(2,1)S(1)}, bf16[256,1024]{1,0:T(8,128)(2,1)S(1)}, u32[]{:S(2)}, u32[]{:S(2)}) collective-permute-start(bf16[256,1024]{1,0:T(8,128)(2,1)S(1)} %pad_maximum_fusion), channel_id=1, source_target_pairs={{0,16},{16,0},{32,48},{48,32},{64,80},{80,64},{96,112},{112,96},{1... | collective-permute-start | bytes 1572872 | tf_op jit(solution)/shard_map/ppermute | solution.py:418
  20.1 18.4 %collective-permute-start.9 = (bf16[128,1024]{1,0:T(8,128)(2,1)S(1)}, bf16[128,1024]{1,0:T(8,128)(2,1)S(1)}, u32[]{:S(2)}, u32[]{:S(2)}) collective-permute-start(bf16[128,1024]{1,0:T(8,128)(2,1)S(1)} %get-tuple-element.52), channel_id=1, source_target_pairs={{0,1},{1,2},{2,3},{3,4},{4,5},{5,6},{6,7},{7,8},{8,9},{9,10},{10,1... | collective-permute-start | bytes 786440 | tf_op jit(solution)/shard_map/ppermute | solution.py:408
  21.4 19.8 %collective-permute-start.10 = (bf16[128,1024]{1,0:T(8,128)(2,1)S(1)}, bf16[128,1024]{1,0:T(8,128)(2,1)S(1)}, u32[]{:S(2)}, u32[]{:S(2)}) collective-permute-start(bf16[128,1024]{1,0:T(8,128)(2,1)S(1)} %get-tuple-element.53), channel_id=1, source_target_pairs={{0,15},{1,0},{2,1},{3,2},{4,3},{5,4},{6,5},{7,6},{8,7},{9,8},{10,9... | collective-permute-start | bytes 786440 | tf_op jit(solution)/shard_map/ppermute | solution.py:409
  26.7 9.3 %collective-permute-start.3 = (bf16[8,1024]{1,0:T(8,128)(2,1)S(1)}, bf16[8,1024]{1,0:T(8,128)(2,1)S(1)}, u32[]{:S(2)}, u32[]{:S(2)}) collective-permute-start(bf16[8,1024]{1,0:T(8,128)(2,1)S(1)} %get-tuple-element.43), channel_id=1, source_target_pairs={{0,32},{16,48},{32,0},{48,16},{64,96},{80,112},{96,64},{112,80},{1... | collective-permute-start | bytes 49160 | tf_op jit(solution)/shard_map/ppermute | solution.py:389
  36.7 5.4 %collective-permute-start.4 = (bf16[64,1024]{1,0:T(8,128)(2,1)S(1)}, bf16[64,1024]{1,0:T(8,128)(2,1)S(1)}, u32[]{:S(2)}, u32[]{:S(2)}) collective-permute-start(bf16[64,1024]{1,0:T(8,128)(2,1)S(1)} %get-tuple-element.45), channel_id=1, source_target_pairs={{0,16},{16,0},{32,48},{48,32},{64,80},{80,64},{96,112},{112,96},{1... | collective-permute-start | bytes 393224 | tf_op jit(solution)/shard_map/ppermute | solution.py:417
  38.0 6.5 %collective-permute-start.5 = (bf16[64,1024]{1,0:T(8,128)(2,1)S(1)}, bf16[64,1024]{1,0:T(8,128)(2,1)S(1)}, u32[]{:S(2)}, u32[]{:S(2)}) collective-permute-start(bf16[64,1024]{1,0:T(8,128)(2,1)S(1)} %get-tuple-element.46), channel_id=1, source_target_pairs={{0,128},{16,144},{32,160},{48,176},{64,192},{80,208},{96,224},{112... | collective-permute-start | bytes 393224 | tf_op jit(solution)/shard_map/ppermute | solution.py:417
  38.5 9.6 %collective-permute-start.6 = (bf16[64,1024]{1,0:T(8,128)(2,1)S(1)}, bf16[64,1024]{1,0:T(8,128)(2,1)S(1)}, u32[]{:S(2)}, u32[]{:S(2)}) collective-permute-start(bf16[64,1024]{1,0:T(8,128)(2,1)S(1)} %get-tuple-element.47), channel_id=1, source_target_pairs={{0,144},{16,128},{32,176},{48,160},{64,208},{80,192},{96,240},{112... | collective-permute-start | bytes 393224 | tf_op jit(solution)/shard_map/ppermute | solution.py:417
  41.2 12.3 %collective-permute-start.11 = (bf16[64,1024]{1,0:T(8,128)(2,1)S(1)}, bf16[64,1024]{1,0:T(8,128)(2,1)S(1)}, u32[]{:S(2)}, u32[]{:S(2)}) collective-permute-start(bf16[64,1024]{1,0:T(8,128)(2,1)S(1)} %get-tuple-element.56), channel_id=1, source_target_pairs={{0,64},{16,80},{32,96},{48,112},{64,128},{80,144},{96,160},{112,17... | collective-permute-start | bytes 393224 | tf_op jit(solution)/shard_map/ppermute | solution.py:417
  42.1 11.5 %collective-permute-start.12 = (bf16[64,1024]{1,0:T(8,128)(2,1)S(1)}, bf16[64,1024]{1,0:T(8,128)(2,1)S(1)}, u32[]{:S(2)}, u32[]{:S(2)}) collective-permute-start(bf16[64,1024]{1,0:T(8,128)(2,1)S(1)} %get-tuple-element.57), channel_id=1, source_target_pairs={{0,80},{16,64},{32,112},{48,96},{64,144},{80,128},{96,176},{112,16... | collective-permute-start | bytes 393224 | tf_op jit(solution)/shard_map/ppermute | solution.py:417
  44.4 9.2 %collective-permute-start.13 = (bf16[64,1024]{1,0:T(8,128)(2,1)S(1)}, bf16[64,1024]{1,0:T(8,128)(2,1)S(1)}, u32[]{:S(2)}, u32[]{:S(2)}) collective-permute-start(bf16[64,1024]{1,0:T(8,128)(2,1)S(1)} %get-tuple-element.58), channel_id=1, source_target_pairs={{0,192},{16,208},{32,224},{48,240},{64,0},{80,16},{96,32},{112,48}... | collective-permute-start | bytes 393224 | tf_op jit(solution)/shard_map/ppermute | solution.py:417
  48.1 5.5 %collective-permute-start.14 = (bf16[64,1024]{1,0:T(8,128)(2,1)S(1)}, bf16[64,1024]{1,0:T(8,128)(2,1)S(1)}, u32[]{:S(2)}, u32[]{:S(2)}) collective-permute-start(bf16[64,1024]{1,0:T(8,128)(2,1)S(1)} %get-tuple-element.59), channel_id=1, source_target_pairs={{0,208},{16,192},{32,240},{48,224},{64,16},{80,0},{96,48},{112,32}... | collective-permute-start | bytes 393224 | tf_op jit(solution)/shard_map/ppermute | solution.py:417
  49.3 4.3 %copy-start.2 = (bf16[1024,1024]{1,0:T(8,128)(2,1)S(1)}, bf16[1024,1024]{1,0:T(8,128)(2,1)}, u32[]{:S(2)}) copy-start(bf16[1024,1024]{1,0:T(8,128)(2,1)} %wo_ref.1) | copy-start | bytes 6291460
  49.3 4.3 %copy-start.4 = (bf16[256,1024]{1,0:T(8,128)(2,1)S(1)}, bf16[256,1024]{1,0:T(8,128)(2,1)}, u32[]{:S(2)}) copy-start(bf16[256,1024]{1,0:T(8,128)(2,1)} %feat_ref.3) | copy-start | bytes 1572868
  49.3 4.4 %copy-start.6 = (s32[2,6]{1,0:T(2,128)S(1)}, s32[2,6]{1,0:T(2,128)}, u32[]{:S(2)}) copy-start(s32[2,6]{1,0:T(2,128)} %peers_hbm.1) | copy-start | bytes 148
  49.3 4.4 %copy-start.7 = (s32[2]{0:T(128)S(1)}, s32[2]{0:T(128)}, u32[]{:S(2)}) copy-start(s32[2]{0:T(128)} %count_hbm.1) | copy-start | bytes 28

commit v2 on v1

--- a/solution.py
+++ b/solution.py
@@ -17,8 +17,8 @@
 PICKS = 8
 SLOTS = 15
 RIM = SLOTS * PORTAL
-FIRST = (1, 2, 3, 4, 5, 6, 7, 8, 9, 12, 13)
-SECOND = (10, 11, 14, 15)
+FIRST = (1, 2, 3, 4, 5, 6, 7, 8, 9, 10, 14)
+SECOND = (11, 15, 12, 13)
 MIB = 1024 * 1024
 SCALE2 = HEAD**-0.5 * 1.4426950408889634
 F32 = jnp.float32
@@ -47,11 +47,15 @@
     return index // 4, (index // 2) % 2, index % 2
 
 
+def normalized(features):
+    widened = features.astype(F32)
+    factor = lax.rsqrt(jnp.mean(widened * widened, axis=1, keepdims=True) + EPSILON)
+    return (widened * factor).astype(BF16)
+
+
 def norm_kernel(feat_ref, a_ref, up_ref, down_ref):
     rows = feat_ref.shape[0]
-    widened = feat_ref[...].astype(F32)
-    factor = lax.rsqrt(jnp.mean(widened * widened, axis=1, keepdims=True) + EPSILON)
-    normed = (widened * factor).astype(BF16)
+    normed = normalized(feat_ref[...])
     a_ref[...] = normed
     down_ref[...] = normed[:TILE]
     up_ref[...] = normed[rows - TILE :]
@@ -77,15 +81,17 @@
     picks_ref[...] = picks.astype(F32).astype(BF16)
 
 
-def relay_kernel(a_ref, picks_ref, *out_refs):
-    rows = a_ref.shape[0]
+def relay_kernel(feat_ref, picks_ref, *refs):
+    out_refs, normed_ref = refs[:-1], refs[-1]
+    rows = feat_ref.shape[0]
+    normed_ref[...] = normalized(feat_ref[...]).astype(F32)
     picks = picks_ref[...].astype(F32)
     for i, ref in enumerate(out_refs):
         pick = jnp.broadcast_to(picks[i : i + 1], (PORTAL, picks.shape[1]))
-        tile = a_ref[:PORTAL].astype(F32)
+        tile = normed_ref[:PORTAL]
         for k in range(1, rows // PORTAL):
             tile = jnp.where(
-                pick == float(k), a_ref[k * PORTAL : (k + 1) * PORTAL].astype(F32), tile
+                pick == float(k), normed_ref[k * PORTAL : (k + 1) * PORTAL], tile
             )
         ref[...] = tile.astype(BF16)
 
@@ -223,7 +229,7 @@
     mine_ref, l1_ref, l4_ref, l5_ref, x1_ref, x2_ref, x3_ref, swap_ref, lo_ref, hi_ref,
     wk_ref, wv_ref, ke_ref, ve_ref, x_s,
 ):
-    tiles = {8: mine_ref[...], 9: l1_ref[...], 12: l4_ref[...], 13: l5_ref[...]}
+    tiles = {8: mine_ref[...], 9: l1_ref[...], 10: l4_ref[...], 14: l5_ref[...]}
     for dx, ref in ((1, x1_ref), (2, x2_ref), (3, x3_ref)):
         tiles[2 * dx] = ref[:PORTAL]
     for i, pos in enumerate((1, 3, 5, 7)):
@@ -366,6 +372,8 @@
     half = shape(TILE, width)
     tile = shape(PORTAL, width)
     square = shape(rows, width)
+    square = shape(rows, width)
+    across = lax.ppermute(features, "grp", moved(0, 1, 0))
     a, up, down = named(
         norm_kernel,
         out_shape=(square, half, half),
@@ -373,7 +381,6 @@
         out_specs=(VMEM,) * 3,
         compiler_params=params(4),
     )(features)
-    across = lax.ppermute(a, "grp", moved(0, 1, 0))
     x1, x2, x3, mate, picks = named(
         pack_kernel,
         out_shape=(tall, tall, tall, tile, shape(PICKS, width)),
@@ -404,7 +411,7 @@
         + stages(rows),
         compiler_params=params(8),
     )(band_reach, a, query_weight, key_weight, value_weight)
-    up, down, queries, x1, x3 = lax.optimization_barrier((up, down, queries, x1, x3))
+    up, down, queries = lax.optimization_barrier((up, down, queries))
     lo = lax.ppermute(up, "rng", [(i, (i + 1) % ranks) for i in range(ranks)])
     hi = lax.ppermute(down, "rng", [(i, (i - 1) % ranks) for i in range(ranks)])
     relayed = named(
@@ -412,6 +419,7 @@
         out_shape=(tile,) * PICKS,
         in_specs=[VMEM] * 2,
         out_specs=(VMEM,) * PICKS,
+        scratch_shapes=[pltpu.VMEM((rows, width), F32)],
         compiler_params=params(4),
     )(across, picks)
     late = {i: lax.ppermute(relayed[i], "grp", moved(i // 2, 0, i % 2)) for i in range(1, PICKS)}
@@ -430,7 +438,7 @@
         scratch_shapes=[pltpu.VMEM((far_rows, width), BF16)],
         compiler_params=params(8),
     )(
-        relayed[0], late[1], late[4], late[5], x1, x2, x3, swapped, lo, hi,
+        relayed[0], late[1], late[2], late[6], x1, x2, x3, swapped, lo, hi,
         key_weight, value_weight,
     )
     span = MAXLONG * PORTAL + TILE
@@ -461,7 +469,7 @@
         compiler_params=params(14),
     )(
         long_peers, long_count, band_reach, queries, acc, top, total, features,
-        far_keys, far_values, late[2], late[3], late[6], late[7], key_weight, value_weight, out_weight,
+        far_keys, far_values, late[3], late[7], late[4], late[5], key_weight, value_weight, out_weight,
     )
     return updated
 

time: 60.3 us -> 60.7 us (level)
  starting transfers between devices: 27.4 us -> 30.5 us
  waiting for transfers between devices: 14.5 us -> 11.9 us
    ppermute x7, starting transfers between devices: 8.59 us -> 11 us  [local(): lax.ppermute(relayed[i], 'grp', moved(i // 2, 0, i % 2))]
    ppermute x7, waiting for transfers between devices: 4.03 us -> 1.96 us  [local(): lax.ppermute(relayed[i], 'grp', moved(i // 2, 0, i % 2))]
where the time goes in v2:
time: 60.7 us; the launch traced here: 60.5 us
  starting transfers between devices  30.5 us (50%)
  Pallas kernels  15.4 us (25%)
  waiting for transfers between devices  11.9 us (20%)
  local copies, waits for them, and re-layouts  1.75 us (3%)
  between operations  0.98 us (2%)
    pallas_call x6, Pallas kernels, run(): return pl.pallas_call(kernel, **kw)(*args)  15.4 us
    ppermute x7, starting transfers between devices, local(): lax.ppermute(relayed[i], 'grp', moved(i // 2, 0, i % 2))  11 us
    ppermute x1, waiting for transfers between devices, local(): picks = lax.ppermute(picks, 'grp', moved(0, 1, 0))  6.69 us
    ppermute x3, starting transfers between devices, local(): lax.ppermute(part, 'grp', moved(dx, 0, 0))  5.71 us
    ppermute x1, starting transfers between devices, local(): hi = lax.ppermute(down, 'rng', [(i, (i - 1) % ranks) for i in range(ranks)])  5.29 us
    ppermute x3, waiting for transfers between devices, local(): lax.ppermute(part, 'grp', moved(dx, 0, 0))  3.24 us
    ppermute x1, starting transfers between devices, local(): across = lax.ppermute(features, 'grp', moved(0, 1, 0))  2.91 us
    ppermute x1, starting transfers between devices, local(): picks = lax.ppermute(picks, 'grp', moved(0, 1, 0))  2.62 us
  transfers between devices with their start and end apart: 15, of which 4 were waited for; matrix products, arithmetic and copies ran while one was open for 0% of the time, Pallas kernels for 14%

profile of v2, /device:TPU:1, one launch (start us, length us, event | category | flops | bytes accessed | tf_op | source)
XLA Modules:
  0.0 60.5 jit_solution(16901927647123646096)
XLA Ops:
  0.0 1.0 %copy-done.3 = bf16[256,1024]{1,0:T(8,128)(2,1)S(1)} copy-done((bf16[256,1024]{1,0:T(8,128)(2,1)S(1)}, bf16[256,1024]{1,0:T(8,128)(2,1)}, u32[]{:S(2)}) %copy-start.3) | copy-done | bytes 524312
  1.0 0.2 shard_map.91
  1.2 0.0 copy-start.8
  1.3 0.6 %copy-done.8 = s32[1,16]{1,0:T(1,128)S(1)} copy-done((s32[1,16]{1,0:T(1,128)S(1)}, s32[1,16]{1,0:T(1,128)}, u32[]{:S(2)}) %copy-start.8) | copy-done | bytes 88
  1.9 0.6 %shard_map.93 = (bf16[128,1024]{1,0:T(8,128)(2,1)S(1)}, bf16[128,1024]{1,0:T(8,128)(2,1)S(1)}, bf16[128,1024]{1,0:T(8,128)(2,1)S(1)}, bf16[64,1024]{1,0:T(8,128)(2,1)S(1)}, bf16[8,1024]{1,0:T(8,128)(2,1)S(1)}) custom-call(s32[1,16]{1,0:T(1,128)S(1)} %copy-done.8, bf16[256,1024]{1,0:T(8,128)(2,1)S(1)} %get-tuple-element.33.a_ref), custom_call_target="tpu_custom_call" | custom-call | flops 10000000000 | bytes 8388608 | tf_op jit(solution)/shard_map/pallas_call | solution.py:352
  2.6 2.1 %collective-permute-start.5 = (bf16[128,1024]{1,0:T(8,128)(2,1)S(1)}, bf16[128,1024]{1,0:T(8,128)(2,1)S(1)}, u32[]{:S(2)}, u32[]{:S(2)}) collective-permute-start(bf16[128,1024]{1,0:T(8,128)(2,1)S(1)} %get-tuple-element.44), channel_id=1, source_target_pairs={{0,64},{16,80},{32,96},{48,112},{64,128},{80,144},{96,160},{112,17... | collective-permute-start | bytes 786440 | tf_op jit(solution)/shard_map/ppermute | solution.py:393
  4.7 2.5 %collective-permute-start.6 = (bf16[128,1024]{1,0:T(8,128)(2,1)S(1)}, bf16[128,1024]{1,0:T(8,128)(2,1)S(1)}, u32[]{:S(2)}, u32[]{:S(2)}) collective-permute-start(bf16[128,1024]{1,0:T(8,128)(2,1)S(1)} %get-tuple-element.45), channel_id=1, source_target_pairs={{0,128},{16,144},{32,160},{48,176},{64,192},{80,208},{96,224},{112... | collective-permute-start | bytes 786440 | tf_op jit(solution)/shard_map/ppermute | solution.py:393
  7.1 1.2 %collective-permute-start.7 = (bf16[128,1024]{1,0:T(8,128)(2,1)S(1)}, bf16[128,1024]{1,0:T(8,128)(2,1)S(1)}, u32[]{:S(2)}, u32[]{:S(2)}) collective-permute-start(bf16[128,1024]{1,0:T(8,128)(2,1)S(1)} %get-tuple-element.46), channel_id=1, source_target_pairs={{0,192},{16,208},{32,224},{48,240},{64,0},{80,16},{96,32},{112,48}... | collective-permute-start | bytes 786440 | tf_op jit(solution)/shard_map/ppermute | solution.py:393
  8.3 2.9 %collective-permute-start = (bf16[256,1024]{1,0:T(8,128)(2,1)S(1)}, bf16[256,1024]{1,0:T(8,128)(2,1)S(1)}, u32[]{:S(2)}, u32[]{:S(2)}) collective-permute-start(bf16[256,1024]{1,0:T(8,128)(2,1)S(1)} %copy-done.4), channel_id=1, source_target_pairs={{0,32},{16,48},{32,0},{48,16},{64,96},{80,112},{96,64},{112,80},{1... | collective-permute-start | bytes 1572872 | tf_op jit(solution)/shard_map/ppermute | solution.py:376
  11.9 3.3 %shard_map.92 = (bf16[256,1024]{1,0:T(8,128)(2,1)S(1)}, f32[256,1024]{1,0:T(8,128)S(1)}, f32[16,256,128]{2,1,0:T(8,128)S(1)}, f32[256,1024]{1,0:T(8,128)S(1)}) custom-call(s32[1]{0:T(128)S(6)} %copy.14.reach_ref, bf16[256,1024]{1,0:T(8,128)(2,1)S(1)} %get-tuple-element.33.a_ref, bf16[1024,1024]{1,0:T(8,128)(2,1)S(1)} %copy-done.5, ...), custom_call_target="tpu_custom_call" | custom-call | tf_op jit(solution)/shard_map/pallas_call | solution.py:352
  15.2 3.2 %collective-permute-done.6.x2_ref = bf16[128,1024]{1,0:T(8,128)(2,1)S(1)} collective-permute-done((bf16[128,1024]{1,0:T(8,128)(2,1)S(1)}, bf16[128,1024]{1,0:T(8,128)(2,1)S(1)}, u32[]{:S(2)}, u32[]{:S(2)}) %collective-permute-start.6) | collective-permute-done | bytes 262176 | tf_op jit(solution)/shard_map/ppermute | solution.py:393
  18.5 0.0 collective-permute-done.7.x3_ref
  18.5 1.6 %collective-permute-start.8 = (bf16[256,1024]{1,0:T(8,128)(2,1)S(1)}, bf16[256,1024]{1,0:T(8,128)(2,1)S(1)}, u32[]{:S(2)}, u32[]{:S(2)}) collective-permute-start(bf16[256,1024]{1,0:T(8,128)(2,1)S(1)} %pad_maximum_fusion), channel_id=1, source_target_pairs={{0,16},{16,0},{32,48},{48,32},{64,80},{80,64},{96,112},{112,96},{1... | collective-permute-start | bytes 1572872 | tf_op jit(solution)/shard_map/ppermute | solution.py:426
  20.2 1.3 %collective-permute-start.9 = (bf16[128,1024]{1,0:T(8,128)(2,1)S(1)}, bf16[128,1024]{1,0:T(8,128)(2,1)S(1)}, u32[]{:S(2)}, u32[]{:S(2)}) collective-permute-start(bf16[128,1024]{1,0:T(8,128)(2,1)S(1)} %get-tuple-element.48), channel_id=1, source_target_pairs={{0,1},{1,2},{2,3},{3,4},{4,5},{5,6},{6,7},{7,8},{8,9},{9,10},{10,1... | collective-permute-start | bytes 786440 | tf_op jit(solution)/shard_map/ppermute | solution.py:415
  21.5 5.3 %collective-permute-start.10 = (bf16[128,1024]{1,0:T(8,128)(2,1)S(1)}, bf16[128,1024]{1,0:T(8,128)(2,1)S(1)}, u32[]{:S(2)}, u32[]{:S(2)}) collective-permute-start(bf16[128,1024]{1,0:T(8,128)(2,1)S(1)} %get-tuple-element.49), channel_id=1, source_target_pairs={{0,15},{1,0},{2,1},{3,2},{4,3},{5,4},{6,5},{7,6},{8,7},{9,8},{10,9... | collective-permute-start | bytes 786440 | tf_op jit(solution)/shard_map/ppermute | solution.py:416
  26.7 2.6 %collective-permute-start.1 = (bf16[8,1024]{1,0:T(8,128)(2,1)S(1)}, bf16[8,1024]{1,0:T(8,128)(2,1)S(1)}, u32[]{:S(2)}, u32[]{:S(2)}) collective-permute-start(bf16[8,1024]{1,0:T(8,128)(2,1)S(1)} %get-tuple-element.39), channel_id=1, source_target_pairs={{0,32},{16,48},{32,0},{48,16},{64,96},{80,112},{96,64},{112,80},{1... | collective-permute-start | bytes 49160 | tf_op jit(solution)/shard_map/ppermute | solution.py:396
  29.4 6.7 %collective-permute-done.1.picks_ref = bf16[8,1024]{1,0:T(8,128)(2,1)S(1)} collective-permute-done((bf16[8,1024]{1,0:T(8,128)(2,1)S(1)}, bf16[8,1024]{1,0:T(8,128)(2,1)S(1)}, u32[]{:S(2)}, u32[]{:S(2)}) %collective-permute-start.1) | collective-permute-done | bytes 16416 | tf_op jit(solution)/shard_map/ppermute | solution.py:396
  36.1 0.6 %shard_map.94 = (bf16[64,1024]{1,0:T(8,128)(2,1)S(1)}, bf16[64,1024]{1,0:T(8,128)(2,1)S(1)}, bf16[64,1024]{1,0:T(8,128)(2,1)S(1)}, bf16[64,1024]{1,0:T(8,128)(2,...) custom-call(bf16[256,1024]{1,0:T(8,128)(2,1)S(1)} %collective-permut, ...), custom_call_target="tpu_custom_call" | custom-call | tf_op jit(solution)/shard_map/pallas_call | solution.py:352
  36.7 1.3 %collective-permute-start.2 = (bf16[64,1024]{1,0:T(8,128)(2,1)S(1)}, bf16[64,1024]{1,0:T(8,128)(2,1)S(1)}, u32[]{:S(2)}, u32[]{:S(2)}) collective-permute-start(bf16[64,1024]{1,0:T(8,128)(2,1)S(1)} %get-tuple-element.41), channel_id=1, source_target_pairs={{0,16},{16,0},{32,48},{48,32},{64,80},{80,64},{96,112},{112,96},{1... | collective-permute-start | bytes 393224 | tf_op jit(solution)/shard_map/ppermute | solution.py:425
  38.0 1.0 %collective-permute-start.3 = (bf16[64,1024]{1,0:T(8,128)(2,1)S(1)}, bf16[64,1024]{1,0:T(8,128)(2,1)S(1)}, u32[]{:S(2)}, u32[]{:S(2)}) collective-permute-start(bf16[64,1024]{1,0:T(8,128)(2,1)S(1)} %get-tuple-element.42), channel_id=1, source_target_pairs={{0,64},{16,80},{32,96},{48,112},{64,128},{80,144},{96,160},{112,17... | collective-permute-start | bytes 393224 | tf_op jit(solution)/shard_map/ppermute | solution.py:425
  39.1 1.6 %collective-permute-start.4 = (bf16[64,1024]{1,0:T(8,128)(2,1)S(1)}, bf16[64,1024]{1,0:T(8,128)(2,1)S(1)}, u32[]{:S(2)}, u32[]{:S(2)}) collective-permute-start(bf16[64,1024]{1,0:T(8,128)(2,1)S(1)} %get-tuple-element.43), channel_id=1, source_target_pairs={{0,192},{16,208},{32,224},{48,240},{64,0},{80,16},{96,32},{112,48}... | collective-permute-start | bytes 393224 | tf_op jit(solution)/shard_map/ppermute | solution.py:425
  40.7 0.4 collective-permute-start.11
  41.1 0.0 collective-permute-done.2.l1_ref
  41.1 2.6 %collective-permute-start.12 = (bf16[64,1024]{1,0:T(8,128)(2,1)S(1)}, bf16[64,1024]{1,0:T(8,128)(2,1)S(1)}, u32[]{:S(2)}, u32[]{:S(2)}) collective-permute-start(bf16[64,1024]{1,0:T(8,128)(2,1)S(1)} %get-tuple-element.53), channel_id=1, source_target_pairs={{0,208},{16,192},{32,240},{48,224},{64,16},{80,0},{96,48},{112,32}... | collective-permute-start | bytes 393224 | tf_op jit(solution)/shard_map/ppermute | solution.py:425
  43.7 0.5 collective-permute-done.3.l4_ref
  44.2 1.1 %collective-permute-start.13 = (bf16[64,1024]{1,0:T(8,128)(2,1)S(1)}, bf16[64,1024]{1,0:T(8,128)(2,1)S(1)}, u32[]{:S(2)}, u32[]{:S(2)}) collective-permute-start(bf16[64,1024]{1,0:T(8,128)(2,1)S(1)} %get-tuple-element.54), channel_id=1, source_target_pairs={{0,128},{16,144},{32,160},{48,176},{64,192},{80,208},{96,224},{112... | collective-permute-start | bytes 393224 | tf_op jit(solution)/shard_map/ppermute | solution.py:425
  45.4 0.0 collective-permute-done.4.l5_ref
  45.4 2.9 %collective-permute-start.14 = (bf16[64,1024]{1,0:T(8,128)(2,1)S(1)}, bf16[64,1024]{1,0:T(8,128)(2,1)S(1)}, u32[]{:S(2)}, u32[]{:S(2)}) collective-permute-start(bf16[64,1024]{1,0:T(8,128)(2,1)S(1)} %get-tuple-element.55), channel_id=1, source_target_pairs={{0,144},{16,128},{32,176},{48,160},{64,208},{80,192},{96,240},{112... | collective-permute-start | bytes 393224 | tf_op jit(solution)/shard_map/ppermute | solution.py:425
  48.3 0.0 collective-permute-done.8.swap_ref
  48.3 4.3 %shard_map.95 = (bf16[1216,1024]{1,0:T(8,128)(2,1)S(1)}, bf16[1216,1024]{1,0:T(8,128)(2,1)S(1)}) custom-call(bf16[64,1024]{1,0:T(8,128)(2,1)S(1)} %get-tuple-element.40.mine_ref, bf16[64,1024]{1,0:T(8,128)(2,1)S(1)} %collective-permute-done.2.l1_ref, bf16[64,1024]{1,0:T(8,128)(2,1)S(1)} %collective-permute-done.3.l4_ref, ...), custom_call_target="tpu_custom_call" | custom-call | tf_op jit(solution)/shard_map/pallas_call | solution.py:352
  52.6 1.4 %collective-permute-done.14.l3 = bf16[64,1024]{1,0:T(8,128)(2,1)S(1)} collective-permute-done((bf16[64,1024]{1,0:T(8,128)(2,1)S(1)}, bf16[64,1024]{1,0:T(8,128)(2,1)S(1)}, u32[]{:S(2)}, u32[]{:S(2)}) %collective-permute-start.14) | collective-permute-done | bytes 131104 | tf_op jit(solution)/shard_map/ppermute | solution.py:425
  54.0 6.3 %shard_map.96 = (bf16[256,1024]{1,0:T(8,128)(2,1)}, bf16[1216,1024]{1,0:T(8,128)(2,1)S(1)}, bf16[1216,1024]{1,0:T(8,128)(2,1)S(1)}) custom-call(s32[2,6]{1,0:T(2,128)S(1)} %copy-done.6, s32[2]{0:T(128)S(1)} %copy-done.7, s32[1]{0:T(128)S(6)} %copy.14.reach_ref, ...), custom_call_target="tpu_custom_call", output_to_operand_aliasing={{1}: (8, {}), {2}: (9, {})} | custom-call | tf_op jit(solution)/shard_map/pallas_call | solution.py:352
  (26 shorter events, 0.1 us)
Async XLA Ops:
  0.0 1.0 %copy-start.3 = (bf16[256,1024]{1,0:T(8,128)(2,1)S(1)}, bf16[256,1024]{1,0:T(8,128)(2,1)}, u32[]{:S(2)}) copy-start(bf16[256,1024]{1,0:T(8,128)(2,1)} %feat_ref.3) | copy-start | bytes 1572868
  1.2 0.7 %copy-start.8 = (s32[1,16]{1,0:T(1,128)S(1)}, s32[1,16]{1,0:T(1,128)}, u32[]{:S(2)}) copy-start(s32[1,16]{1,0:T(1,128)} %send_ref.1) | copy-start | bytes 196
  1.9 6.4 %copy-start.4 = (bf16[256,1024]{1,0:T(8,128)(2,1)S(1)}, bf16[256,1024]{1,0:T(8,128)(2,1)}, u32[]{:S(2)}) copy-start(bf16[256,1024]{1,0:T(8,128)(2,1)} %feat_ref.3) | copy-start | bytes 1572868
  1.9 9.9 %copy-start = (bf16[1024,1024]{1,0:T(8,128)(2,1)S(1)}, bf16[1024,1024]{1,0:T(8,128)(2,1)}, u32[]{:S(2)}) copy-start(bf16[1024,1024]{1,0:T(8,128)(2,1)} %wk_ref.5) | copy-start | bytes 6291460
  1.9 9.9 %copy-start.1 = (bf16[1024,1024]{1,0:T(8,128)(2,1)S(1)}, bf16[1024,1024]{1,0:T(8,128)(2,1)}, u32[]{:S(2)}) copy-start(bf16[1024,1024]{1,0:T(8,128)(2,1)} %wv_ref.5) | copy-start | bytes 6291460
  1.9 9.9 %copy-start.5 = (bf16[1024,1024]{1,0:T(8,128)(2,1)S(1)}, bf16[1024,1024]{1,0:T(8,128)(2,1)}, u32[]{:S(2)}) copy-start(bf16[1024,1024]{1,0:T(8,128)(2,1)} %wq_ref.1) | copy-start | bytes 6291460
  2.6 12.6 %collective-permute-start.5 = (bf16[128,1024]{1,0:T(8,128)(2,1)S(1)}, bf16[128,1024]{1,0:T(8,128)(2,1)S(1)}, u32[]{:S(2)}, u32[]{:S(2)}) collective-permute-start(bf16[128,1024]{1,0:T(8,128)(2,1)S(1)} %get-tuple-element.44), channel_id=1, source_target_pairs={{0,64},{16,80},{32,96},{48,112},{64,128},{80,144},{96,160},{112,17... | collective-permute-start | bytes 786440 | tf_op jit(solution)/shard_map/ppermute | solution.py:393
  4.7 13.8 %collective-permute-start.6 = (bf16[128,1024]{1,0:T(8,128)(2,1)S(1)}, bf16[128,1024]{1,0:T(8,128)(2,1)S(1)}, u32[]{:S(2)}, u32[]{:S(2)}) collective-permute-start(bf16[128,1024]{1,0:T(8,128)(2,1)S(1)} %get-tuple-element.45), channel_id=1, source_target_pairs={{0,128},{16,144},{32,160},{48,176},{64,192},{80,208},{96,224},{112... | collective-permute-start | bytes 786440 | tf_op jit(solution)/shard_map/ppermute | solution.py:393
  7.1 11.4 %collective-permute-start.7 = (bf16[128,1024]{1,0:T(8,128)(2,1)S(1)}, bf16[128,1024]{1,0:T(8,128)(2,1)S(1)}, u32[]{:S(2)}, u32[]{:S(2)}) collective-permute-start(bf16[128,1024]{1,0:T(8,128)(2,1)S(1)} %get-tuple-element.46), channel_id=1, source_target_pairs={{0,192},{16,208},{32,224},{48,240},{64,0},{80,16},{96,32},{112,48}... | collective-permute-start | bytes 786440 | tf_op jit(solution)/shard_map/ppermute | solution.py:393
  8.3 27.8 %collective-permute-start = (bf16[256,1024]{1,0:T(8,128)(2,1)S(1)}, bf16[256,1024]{1,0:T(8,128)(2,1)S(1)}, u32[]{:S(2)}, u32[]{:S(2)}) collective-permute-start(bf16[256,1024]{1,0:T(8,128)(2,1)S(1)} %copy-done.4), channel_id=1, source_target_pairs={{0,32},{16,48},{32,0},{48,16},{64,96},{80,112},{96,64},{112,80},{1... | collective-permute-start | bytes 1572872 | tf_op jit(solution)/shard_map/ppermute | solution.py:376
  18.5 29.8 %collective-permute-start.8 = (bf16[256,1024]{1,0:T(8,128)(2,1)S(1)}, bf16[256,1024]{1,0:T(8,128)(2,1)S(1)}, u32[]{:S(2)}, u32[]{:S(2)}) collective-permute-start(bf16[256,1024]{1,0:T(8,128)(2,1)S(1)} %pad_maximum_fusion), channel_id=1, source_target_pairs={{0,16},{16,0},{32,48},{48,32},{64,80},{80,64},{96,112},{112,96},{1... | collective-permute-start | bytes 1572872 | tf_op jit(solution)/shard_map/ppermute | solution.py:426
  20.2 18.9 %collective-permute-start.9 = (bf16[128,1024]{1,0:T(8,128)(2,1)S(1)}, bf16[128,1024]{1,0:T(8,128)(2,1)S(1)}, u32[]{:S(2)}, u32[]{:S(2)}) collective-permute-start(bf16[128,1024]{1,0:T(8,128)(2,1)S(1)} %get-tuple-element.48), channel_id=1, source_target_pairs={{0,1},{1,2},{2,3},{3,4},{4,5},{5,6},{6,7},{7,8},{8,9},{9,10},{10,1... | collective-permute-start | bytes 786440 | tf_op jit(solution)/shard_map/ppermute | solution.py:415
  21.5 19.3 %collective-permute-start.10 = (bf16[128,1024]{1,0:T(8,128)(2,1)S(1)}, bf16[128,1024]{1,0:T(8,128)(2,1)S(1)}, u32[]{:S(2)}, u32[]{:S(2)}) collective-permute-start(bf16[128,1024]{1,0:T(8,128)(2,1)S(1)} %get-tuple-element.49), channel_id=1, source_target_pairs={{0,15},{1,0},{2,1},{3,2},{4,3},{5,4},{6,5},{7,6},{8,7},{9,8},{10,9... | collective-permute-start | bytes 786440 | tf_op jit(solution)/shard_map/ppermute | solution.py:416
  26.7 9.3 %collective-permute-start.1 = (bf16[8,1024]{1,0:T(8,128)(2,1)S(1)}, bf16[8,1024]{1,0:T(8,128)(2,1)S(1)}, u32[]{:S(2)}, u32[]{:S(2)}) collective-permute-start(bf16[8,1024]{1,0:T(8,128)(2,1)S(1)} %get-tuple-element.39), channel_id=1, source_target_pairs={{0,32},{16,48},{32,0},{48,16},{64,96},{80,112},{96,64},{112,80},{1... | collective-permute-start | bytes 49160 | tf_op jit(solution)/shard_map/ppermute | solution.py:396
  36.7 4.4 %collective-permute-start.2 = (bf16[64,1024]{1,0:T(8,128)(2,1)S(1)}, bf16[64,1024]{1,0:T(8,128)(2,1)S(1)}, u32[]{:S(2)}, u32[]{:S(2)}) collective-permute-start(bf16[64,1024]{1,0:T(8,128)(2,1)S(1)} %get-tuple-element.41), channel_id=1, source_target_pairs={{0,16},{16,0},{32,48},{48,32},{64,80},{80,64},{96,112},{112,96},{1... | collective-permute-start | bytes 393224 | tf_op jit(solution)/shard_map/ppermute | solution.py:425
  38.0 6.2 %collective-permute-start.3 = (bf16[64,1024]{1,0:T(8,128)(2,1)S(1)}, bf16[64,1024]{1,0:T(8,128)(2,1)S(1)}, u32[]{:S(2)}, u32[]{:S(2)}) collective-permute-start(bf16[64,1024]{1,0:T(8,128)(2,1)S(1)} %get-tuple-element.42), channel_id=1, source_target_pairs={{0,64},{16,80},{32,96},{48,112},{64,128},{80,144},{96,160},{112,17... | collective-permute-start | bytes 393224 | tf_op jit(solution)/shard_map/ppermute | solution.py:425
  39.1 6.3 %collective-permute-start.4 = (bf16[64,1024]{1,0:T(8,128)(2,1)S(1)}, bf16[64,1024]{1,0:T(8,128)(2,1)S(1)}, u32[]{:S(2)}, u32[]{:S(2)}) collective-permute-start(bf16[64,1024]{1,0:T(8,128)(2,1)S(1)} %get-tuple-element.43), channel_id=1, source_target_pairs={{0,192},{16,208},{32,224},{48,240},{64,0},{80,16},{96,32},{112,48}... | collective-permute-start | bytes 393224 | tf_op jit(solution)/shard_map/ppermute | solution.py:425
  40.7 11.9 %collective-permute-start.11 = (bf16[64,1024]{1,0:T(8,128)(2,1)S(1)}, bf16[64,1024]{1,0:T(8,128)(2,1)S(1)}, u32[]{:S(2)}, u32[]{:S(2)}) collective-permute-start(bf16[64,1024]{1,0:T(8,128)(2,1)S(1)} %get-tuple-element.52), channel_id=1, source_target_pairs={{0,80},{16,64},{32,112},{48,96},{64,144},{80,128},{96,176},{112,16... | collective-permute-start | bytes 393224 | tf_op jit(solution)/shard_map/ppermute | solution.py:425
  41.1 11.5 %collective-permute-start.12 = (bf16[64,1024]{1,0:T(8,128)(2,1)S(1)}, bf16[64,1024]{1,0:T(8,128)(2,1)S(1)}, u32[]{:S(2)}, u32[]{:S(2)}) collective-permute-start(bf16[64,1024]{1,0:T(8,128)(2,1)S(1)} %get-tuple-element.53), channel_id=1, source_target_pairs={{0,208},{16,192},{32,240},{48,224},{64,16},{80,0},{96,48},{112,32}... | collective-permute-start | bytes 393224 | tf_op jit(solution)/shard_map/ppermute | solution.py:425
  44.2 8.4 %collective-permute-start.13 = (bf16[64,1024]{1,0:T(8,128)(2,1)S(1)}, bf16[64,1024]{1,0:T(8,128)(2,1)S(1)}, u32[]{:S(2)}, u32[]{:S(2)}) collective-permute-start(bf16[64,1024]{1,0:T(8,128)(2,1)S(1)} %get-tuple-element.54), channel_id=1, source_target_pairs={{0,128},{16,144},{32,160},{48,176},{64,192},{80,208},{96,224},{112... | collective-permute-start | bytes 393224 | tf_op jit(solution)/shard_map/ppermute | solution.py:425
  45.4 8.7 %collective-permute-start.14 = (bf16[64,1024]{1,0:T(8,128)(2,1)S(1)}, bf16[64,1024]{1,0:T(8,128)(2,1)S(1)}, u32[]{:S(2)}, u32[]{:S(2)}) collective-permute-start(bf16[64,1024]{1,0:T(8,128)(2,1)S(1)} %get-tuple-element.55), channel_id=1, source_target_pairs={{0,144},{16,128},{32,176},{48,160},{64,208},{80,192},{96,240},{112... | collective-permute-start | bytes 393224 | tf_op jit(solution)/shard_map/ppermute | solution.py:425
  48.3 5.7 %copy-start.2 = (bf16[1024,1024]{1,0:T(8,128)(2,1)S(1)}, bf16[1024,1024]{1,0:T(8,128)(2,1)}, u32[]{:S(2)}) copy-start(bf16[1024,1024]{1,0:T(8,128)(2,1)} %wo_ref.1) | copy-start | bytes 6291460
  48.3 5.7 %copy-start.6 = (s32[2,6]{1,0:T(2,128)S(1)}, s32[2,6]{1,0:T(2,128)}, u32[]{:S(2)}) copy-start(s32[2,6]{1,0:T(2,128)} %peers_hbm.1) | copy-start | bytes 148
  48.3 5.7 %copy-start.7 = (s32[2]{0:T(128)S(1)}, s32[2]{0:T(128)}, u32[]{:S(2)}) copy-start(s32[2]{0:T(128)} %count_hbm.1) | copy-start | bytes 28

commit v3 on v2

--- a/solution.py
+++ b/solution.py
@@ -84,16 +84,16 @@
 def relay_kernel(feat_ref, picks_ref, *refs):
     out_refs, normed_ref = refs[:-1], refs[-1]
     rows = feat_ref.shape[0]
-    normed_ref[...] = normalized(feat_ref[...]).astype(F32)
-    picks = picks_ref[...].astype(F32)
+    normed_ref[...] = normalized(feat_ref[...])
+    picks = picks_ref[...]
     for i, ref in enumerate(out_refs):
         pick = jnp.broadcast_to(picks[i : i + 1], (PORTAL, picks.shape[1]))
         tile = normed_ref[:PORTAL]
         for k in range(1, rows // PORTAL):
             tile = jnp.where(
-                pick == float(k), normed_ref[k * PORTAL : (k + 1) * PORTAL], tile
+                pick == jnp.asarray(k, BF16), normed_ref[k * PORTAL : (k + 1) * PORTAL], tile
             )
-        ref[...] = tile.astype(BF16)
+        ref[...] = tile
 
 
 def dot(x, w):
@@ -226,13 +226,13 @@
 
 
 def far_kernel(
-    mine_ref, l1_ref, l4_ref, l5_ref, x1_ref, x2_ref, x3_ref, swap_ref, lo_ref, hi_ref,
+    mine_ref, l4_ref, l5_ref, x1_ref, x2_ref, x3_ref, swap_ref, lo_ref, hi_ref,
     wk_ref, wv_ref, ke_ref, ve_ref, x_s,
 ):
-    tiles = {8: mine_ref[...], 9: l1_ref[...], 10: l4_ref[...], 14: l5_ref[...]}
+    tiles = {8: mine_ref[...], 10: l4_ref[...], 14: l5_ref[...]}
     for dx, ref in ((1, x1_ref), (2, x2_ref), (3, x3_ref)):
         tiles[2 * dx] = ref[:PORTAL]
-    for i, pos in enumerate((1, 3, 5, 7)):
+    for i, pos in enumerate((1, 3, 5, 7, 9)):
         tiles[pos] = swap_ref[i * PORTAL : (i + 1) * PORTAL]
     for i, pos in enumerate(FIRST):
         x_s[tile_rows(i + 1)] = tiles[pos]
@@ -419,12 +419,12 @@
         out_shape=(tile,) * PICKS,
         in_specs=[VMEM] * 2,
         out_specs=(VMEM,) * PICKS,
-        scratch_shapes=[pltpu.VMEM((rows, width), F32)],
+        scratch_shapes=[pltpu.VMEM((rows, width), BF16)],
         compiler_params=params(4),
     )(across, picks)
-    late = {i: lax.ppermute(relayed[i], "grp", moved(i // 2, 0, i % 2)) for i in range(1, PICKS)}
+    late = {i: lax.ppermute(relayed[i], "grp", moved(i // 2, 0, i % 2)) for i in range(2, PICKS)}
     swapped = lax.ppermute(
-        jnp.concatenate([mate, x1[PORTAL:], x2[PORTAL:], x3[PORTAL:]], axis=0),
+        jnp.concatenate([mate, x1[PORTAL:], x2[PORTAL:], x3[PORTAL:], relayed[1]], axis=0),
         "grp",
         moved(0, 0, 1),
     )
@@ -433,12 +433,12 @@
     far_keys, far_values = named(
         far_kernel,
         out_shape=(far, far),
-        in_specs=[VMEM] * 12,
+        in_specs=[VMEM] * 11,
         out_specs=(VMEM,) * 2,
         scratch_shapes=[pltpu.VMEM((far_rows, width), BF16)],
         compiler_params=params(8),
     )(
-        relayed[0], late[1], late[2], late[6], x1, x2, x3, swapped, lo, hi,
+        relayed[0], late[2], late[6], x1, x2, x3, swapped, lo, hi,
         key_weight, value_weight,
     )
     span = MAXLONG * PORTAL + TILE

time: 60.7 us -> 61.6 us (1.015)
  waiting for transfers between devices: 11.9 us -> 15.7 us
  starting transfers between devices: 30.5 us -> 27.8 us
    ppermute x1, waiting for transfers between devices: 6.69 us -> 0.01 us  [local(): picks = lax.ppermute(picks, 'grp', moved(0, 1, 0))]
    ppermute x3, waiting for transfers between devices: 3.24 us -> 8.98 us  [local(): lax.ppermute(part, 'grp', moved(dx, 0, 0))]
    ppermute x1, waiting for transfers between devices: 0.01 us -> 3.95 us  [local(): lo = lax.ppermute(up, 'rng', [(i, (i + 1) % ranks) for i in range(ranks)])]
    ppermute x1, starting transfers between devices: 2.62 us -> 0.06 us  [local(): picks = lax.ppermute(picks, 'grp', moved(0, 1, 0))]
    ppermute x7 -> x6, starting transfers between devices: 11 us -> 9.87 us  [local(): lax.ppermute(relayed[i], 'grp', moved(i // 2, 0, i % 2))]
    ppermute x1, starting transfers between devices: 1.62 us -> 2.48 us  [local(): lax.ppermute(jnp.concatenate([mate, x1[PORTAL:], x2[PORTAL:], x3[PORTAL:]...]
    ppermute x7 -> x6, waiting for transfers between devices: 1.96 us -> 2.75 us  [local(): lax.ppermute(relayed[i], 'grp', moved(i // 2, 0, i % 2))]
    unnamed x18 -> x22, local copies, waits for them, and re-layouts: 1.72 us -> 1.76 us
  transfers between devices with their start and end apart: 15 -> 14, of which waited for: 4 -> 5; matrix products, arithmetic and copies ran while one was open for 0% -> 0% of each run, Pallas kernels for 14% -> 12%
where the time goes in v3:
time: 61.6 us; the launch traced here: 61.5 us
  starting transfers between devices  27.8 us (45%)
  waiting for transfers between devices  15.7 us (25%)
  Pallas kernels  15.2 us (25%)
  local copies, waits for them, and re-layouts  1.77 us (3%)
  between operations  0.97 us (2%)
    pallas_call x6, Pallas kernels, run(): return pl.pallas_call(kernel, **kw)(*args)  15.2 us
    ppermute x6, starting transfers between devices, local(): lax.ppermute(relayed[i], 'grp', moved(i // 2, 0, i % 2))  9.87 us
    ppermute x3, waiting for transfers between devices, local(): lax.ppermute(part, 'grp', moved(dx, 0, 0))  8.98 us
    ppermute x3, starting transfers between devices, local(): lax.ppermute(part, 'grp', moved(dx, 0, 0))  5.71 us
    ppermute x1, starting transfers between devices, local(): hi = lax.ppermute(down, 'rng', [(i, (i - 1) % ranks) for i in range(ranks)])  5.37 us
    ppermute x1, waiting for transfers between devices, local(): lo = lax.ppermute(up, 'rng', [(i, (i + 1) % ranks) for i in range(ranks)])  3.95 us
    ppermute x1, starting transfers between devices, local(): across = lax.ppermute(features, 'grp', moved(0, 1, 0))  2.91 us
    ppermute x6, waiting for transfers between devices, local(): lax.ppermute(relayed[i], 'grp', moved(i // 2, 0, i % 2))  2.75 us
  transfers between devices with their start and end apart: 14, of which 5 were waited for; matrix products, arithmetic and copies ran while one was open for 0% of the time, Pallas kernels for 12%

profile of v3, /device:TPU:1, one launch (start us, length us, event | category | flops | bytes accessed | tf_op | source)
XLA Modules:
  0.0 61.5 jit_solution(12078825469072064605)
XLA Ops:
  0.0 1.0 %copy-done.3 = bf16[256,1024]{1,0:T(8,128)(2,1)S(1)} copy-done((bf16[256,1024]{1,0:T(8,128)(2,1)S(1)}, bf16[256,1024]{1,0:T(8,128)(2,1)}, u32[]{:S(2)}) %copy-start.3) | copy-done | bytes 524312
  1.0 0.2 shard_map.91
  1.2 0.0 copy-start.8
  1.3 0.6 %copy-done.8 = s32[1,16]{1,0:T(1,128)S(1)} copy-done((s32[1,16]{1,0:T(1,128)S(1)}, s32[1,16]{1,0:T(1,128)}, u32[]{:S(2)}) %copy-start.8) | copy-done | bytes 88
  1.9 0.6 %shard_map.93 = (bf16[128,1024]{1,0:T(8,128)(2,1)S(1)}, bf16[128,1024]{1,0:T(8,128)(2,1)S(1)}, bf16[128,1024]{1,0:T(8,128)(2,1)S(1)}, bf16[64,1024]{1,0:T(8,128)(2,1)S(1)}, bf16[8,1024]{1,0:T(8,128)(2,1)S(1)}) custom-call(s32[1,16]{1,0:T(1,128)S(1)} %copy-done.8, bf16[256,1024]{1,0:T(8,128)(2,1)S(1)} %get-tuple-element.33.a_ref), custom_call_target="tpu_custom_call" | custom-call | flops 10000000000 | bytes 8388608 | tf_op jit(solution)/shard_map/pallas_call | solution.py:352
  2.6 2.1 %collective-permute-start.4 = (bf16[128,1024]{1,0:T(8,128)(2,1)S(1)}, bf16[128,1024]{1,0:T(8,128)(2,1)S(1)}, u32[]{:S(2)}, u32[]{:S(2)}) collective-permute-start(bf16[128,1024]{1,0:T(8,128)(2,1)S(1)} %get-tuple-element.43), channel_id=1, source_target_pairs={{0,64},{16,80},{32,96},{48,112},{64,128},{80,144},{96,160},{112,17... | collective-permute-start | bytes 786440 | tf_op jit(solution)/shard_map/ppermute | solution.py:393
  4.7 2.9 %collective-permute-start = (bf16[256,1024]{1,0:T(8,128)(2,1)S(1)}, bf16[256,1024]{1,0:T(8,128)(2,1)S(1)}, u32[]{:S(2)}, u32[]{:S(2)}) collective-permute-start(bf16[256,1024]{1,0:T(8,128)(2,1)S(1)} %copy-done.4), channel_id=1, source_target_pairs={{0,32},{16,48},{32,0},{48,16},{64,96},{80,112},{96,64},{112,80},{1... | collective-permute-start | bytes 1572872 | tf_op jit(solution)/shard_map/ppermute | solution.py:376
  7.6 0.1 collective-permute-start.1
  7.6 2.5 %collective-permute-start.5 = (bf16[128,1024]{1,0:T(8,128)(2,1)S(1)}, bf16[128,1024]{1,0:T(8,128)(2,1)S(1)}, u32[]{:S(2)}, u32[]{:S(2)}) collective-permute-start(bf16[128,1024]{1,0:T(8,128)(2,1)S(1)} %get-tuple-element.44), channel_id=1, source_target_pairs={{0,128},{16,144},{32,160},{48,176},{64,192},{80,208},{96,224},{112... | collective-permute-start | bytes 786440 | tf_op jit(solution)/shard_map/ppermute | solution.py:393
  10.1 1.2 %collective-permute-start.6 = (bf16[128,1024]{1,0:T(8,128)(2,1)S(1)}, bf16[128,1024]{1,0:T(8,128)(2,1)S(1)}, u32[]{:S(2)}, u32[]{:S(2)}) collective-permute-start(bf16[128,1024]{1,0:T(8,128)(2,1)S(1)} %get-tuple-element.45), channel_id=1, source_target_pairs={{0,192},{16,208},{32,224},{48,240},{64,0},{80,16},{96,32},{112,48}... | collective-permute-start | bytes 786440 | tf_op jit(solution)/shard_map/ppermute | solution.py:393
  11.2 0.0 collective-permute-done.4.x1_ref
  11.3 7.2 %collective-permute-done.5.x2_ref = bf16[128,1024]{1,0:T(8,128)(2,1)S(1)} collective-permute-done((bf16[128,1024]{1,0:T(8,128)(2,1)S(1)}, bf16[128,1024]{1,0:T(8,128)(2,1)S(1)}, u32[]{:S(2)}, u32[]{:S(2)}) %collective-permute-start.5) | collective-permute-done | bytes 262176 | tf_op jit(solution)/shard_map/ppermute | solution.py:393
  18.5 1.8 %collective-permute-done.6.x3_ref = bf16[128,1024]{1,0:T(8,128)(2,1)S(1)} collective-permute-done((bf16[128,1024]{1,0:T(8,128)(2,1)S(1)}, bf16[128,1024]{1,0:T(8,128)(2,1)S(1)}, u32[]{:S(2)}, u32[]{:S(2)}) %collective-permute-start.6) | collective-permute-done | bytes 262176 | tf_op jit(solution)/shard_map/ppermute | solution.py:393
  20.3 0.0 collective-permute-done.1.picks_ref
  20.3 0.0 collective-permute-done.feat_ref
  20.3 0.5 shard_map.94
  20.8 2.5 %collective-permute-start.7 = (bf16[320,1024]{1,0:T(8,128)(2,1)S(1)}, bf16[320,1024]{1,0:T(8,128)(2,1)S(1)}, u32[]{:S(2)}, u32[]{:S(2)}) collective-permute-start(bf16[320,1024]{1,0:T(8,128)(2,1)S(1)} %constant_dynamic-update-slice_fusion), channel_id=1, source_target_pairs={{0,16},{16,0},{32,48},{48,32},{64,80},{80,64},{96,112},{112,96},{1... | collective-permute-start | bytes 1966088 | tf_op jit(solution)/shard_map/ppermute | solution.py:426
  24.0 3.4 %shard_map.92 = (bf16[256,1024]{1,0:T(8,128)(2,1)S(1)}, f32[256,1024]{1,0:T(8,128)S(1)}, f32[16,256,128]{2,1,0:T(8,128)S(1)}, f32[256,1024]{1,0:T(8,128)S(1)}) custom-call(s32[1]{0:T(128)S(6)} %copy.18.reach_ref, bf16[256,1024]{1,0:T(8,128)(2,1)S(1)} %get-tuple-element.33.a_ref, bf16[1024,1024]{1,0:T(8,128)(2,1)S(1)} %copy-done.5, ...), custom_call_target="tpu_custom_call" | custom-call | tf_op jit(solution)/shard_map/pallas_call | solution.py:352
  27.3 1.4 %collective-permute-start.8 = (bf16[128,1024]{1,0:T(8,128)(2,1)S(1)}, bf16[128,1024]{1,0:T(8,128)(2,1)S(1)}, u32[]{:S(2)}, u32[]{:S(2)}) collective-permute-start(bf16[128,1024]{1,0:T(8,128)(2,1)S(1)} %get-tuple-element.48), channel_id=1, source_target_pairs={{0,1},{1,2},{2,3},{3,4},{4,5},{5,6},{6,7},{7,8},{8,9},{9,10},{10,1... | collective-permute-start | bytes 786440 | tf_op jit(solution)/shard_map/ppermute | solution.py:415
  28.7 5.4 %collective-permute-start.9 = (bf16[128,1024]{1,0:T(8,128)(2,1)S(1)}, bf16[128,1024]{1,0:T(8,128)(2,1)S(1)}, u32[]{:S(2)}, u32[]{:S(2)}) collective-permute-start(bf16[128,1024]{1,0:T(8,128)(2,1)S(1)} %get-tuple-element.49), channel_id=1, source_target_pairs={{0,15},{1,0},{2,1},{3,2},{4,3},{5,4},{6,5},{7,6},{8,7},{9,8},{10,9... | collective-permute-start | bytes 786440 | tf_op jit(solution)/shard_map/ppermute | solution.py:416
  34.1 1.4 %collective-permute-start.2 = (bf16[64,1024]{1,0:T(8,128)(2,1)S(1)}, bf16[64,1024]{1,0:T(8,128)(2,1)S(1)}, u32[]{:S(2)}, u32[]{:S(2)}) collective-permute-start(bf16[64,1024]{1,0:T(8,128)(2,1)S(1)} %get-tuple-element.41), channel_id=1, source_target_pairs={{0,64},{16,80},{32,96},{48,112},{64,128},{80,144},{96,160},{112,17... | collective-permute-start | bytes 393224 | tf_op jit(solution)/shard_map/ppermute | solution.py:425
  35.5 1.3 %collective-permute-start.3 = (bf16[64,1024]{1,0:T(8,128)(2,1)S(1)}, bf16[64,1024]{1,0:T(8,128)(2,1)S(1)}, u32[]{:S(2)}, u32[]{:S(2)}) collective-permute-start(bf16[64,1024]{1,0:T(8,128)(2,1)S(1)} %get-tuple-element.42), channel_id=1, source_target_pairs={{0,192},{16,208},{32,224},{48,240},{64,0},{80,16},{96,32},{112,48}... | collective-permute-start | bytes 393224 | tf_op jit(solution)/shard_map/ppermute | solution.py:425
  36.8 3.9 %collective-permute-done.8.lo_ref = bf16[128,1024]{1,0:T(8,128)(2,1)S(1)} collective-permute-done((bf16[128,1024]{1,0:T(8,128)(2,1)S(1)}, bf16[128,1024]{1,0:T(8,128)(2,1)S(1)}, u32[]{:S(2)}, u32[]{:S(2)}) %collective-permute-start.8) | collective-permute-done | bytes 262176 | tf_op jit(solution)/shard_map/ppermute | solution.py:415
  40.7 2.0 %collective-permute-start.10 = (bf16[64,1024]{1,0:T(8,128)(2,1)S(1)}, bf16[64,1024]{1,0:T(8,128)(2,1)S(1)}, u32[]{:S(2)}, u32[]{:S(2)}) collective-permute-start(bf16[64,1024]{1,0:T(8,128)(2,1)S(1)} %get-tuple-element.52), channel_id=1, source_target_pairs={{0,80},{16,64},{32,112},{48,96},{64,144},{80,128},{96,176},{112,16... | collective-permute-start | bytes 393224 | tf_op jit(solution)/shard_map/ppermute | solution.py:425
  42.7 0.0 collective-permute-done.9.hi_ref
  42.7 2.7 %collective-permute-start.11 = (bf16[64,1024]{1,0:T(8,128)(2,1)S(1)}, bf16[64,1024]{1,0:T(8,128)(2,1)S(1)}, u32[]{:S(2)}, u32[]{:S(2)}) collective-permute-start(bf16[64,1024]{1,0:T(8,128)(2,1)S(1)} %get-tuple-element.53), channel_id=1, source_target_pairs={{0,208},{16,192},{32,240},{48,224},{64,16},{80,0},{96,48},{112,32}... | collective-permute-start | bytes 393224 | tf_op jit(solution)/shard_map/ppermute | solution.py:425
  45.4 0.9 %collective-permute-start.12 = (bf16[64,1024]{1,0:T(8,128)(2,1)S(1)}, bf16[64,1024]{1,0:T(8,128)(2,1)S(1)}, u32[]{:S(2)}, u32[]{:S(2)}) collective-permute-start(bf16[64,1024]{1,0:T(8,128)(2,1)S(1)} %get-tuple-element.54), channel_id=1, source_target_pairs={{0,128},{16,144},{32,160},{48,176},{64,192},{80,208},{96,224},{112... | collective-permute-start | bytes 393224 | tf_op jit(solution)/shard_map/ppermute | solution.py:425
  46.2 1.7 %collective-permute-start.13 = (bf16[64,1024]{1,0:T(8,128)(2,1)S(1)}, bf16[64,1024]{1,0:T(8,128)(2,1)S(1)}, u32[]{:S(2)}, u32[]{:S(2)}) collective-permute-start(bf16[64,1024]{1,0:T(8,128)(2,1)S(1)} %get-tuple-element.55), channel_id=1, source_target_pairs={{0,144},{16,128},{32,176},{48,160},{64,208},{80,192},{96,240},{112... | collective-permute-start | bytes 393224 | tf_op jit(solution)/shard_map/ppermute | solution.py:425
  48.0 4.3 %shard_map.95 = (bf16[1216,1024]{1,0:T(8,128)(2,1)S(1)}, bf16[1216,1024]{1,0:T(8,128)(2,1)S(1)}) custom-call(bf16[64,1024]{1,0:T(8,128)(2,1)S(1)} %get-tuple-element.40.mine_ref, bf16[64,1024]{1,0:T(8,128)(2,1)S(1)} %collective-permute-done.2.l4_ref, bf16[64,1024]{1,0:T(8,128)(2,1)S(1)} %collective-permute-done.3.l5_ref, ...), custom_call_target="tpu_custom_call" | custom-call | tf_op jit(solution)/shard_map/pallas_call | solution.py:352
  52.2 1.7 %collective-permute-done.11.l1 = bf16[64,1024]{1,0:T(8,128)(2,1)S(1)} collective-permute-done((bf16[64,1024]{1,0:T(8,128)(2,1)S(1)}, bf16[64,1024]{1,0:T(8,128)(2,1)S(1)}, u32[]{:S(2)}, u32[]{:S(2)}) %collective-permute-start.11) | collective-permute-done | bytes 131104 | tf_op jit(solution)/shard_map/ppermute | solution.py:425
  53.9 1.1 %collective-permute-done.13.l3 = bf16[64,1024]{1,0:T(8,128)(2,1)S(1)} collective-permute-done((bf16[64,1024]{1,0:T(8,128)(2,1)S(1)}, bf16[64,1024]{1,0:T(8,128)(2,1)S(1)}, u32[]{:S(2)}, u32[]{:S(2)}) %collective-permute-start.13) | collective-permute-done | bytes 131104 | tf_op jit(solution)/shard_map/ppermute | solution.py:425
  55.0 6.3 %shard_map.96 = (bf16[256,1024]{1,0:T(8,128)(2,1)}, bf16[1216,1024]{1,0:T(8,128)(2,1)S(1)}, bf16[1216,1024]{1,0:T(8,128)(2,1)S(1)}) custom-call(s32[2,6]{1,0:T(2,128)S(1)} %copy-done.6, s32[2]{0:T(128)S(1)} %copy-done.7, s32[1]{0:T(128)S(6)} %copy.18.reach_ref, ...), custom_call_target="tpu_custom_call", output_to_operand_aliasing={{1}: (8, {}), {2}: (9, {})} | custom-call | tf_op jit(solution)/shard_map/pallas_call | solution.py:352
  (25 shorter events, 0.1 us)
Async XLA Ops:
  0.0 1.0 %copy-start.3 = (bf16[256,1024]{1,0:T(8,128)(2,1)S(1)}, bf16[256,1024]{1,0:T(8,128)(2,1)}, u32[]{:S(2)}) copy-start(bf16[256,1024]{1,0:T(8,128)(2,1)} %feat_ref.3) | copy-start | bytes 1572868
  1.2 0.7 %copy-start.8 = (s32[1,16]{1,0:T(1,128)S(1)}, s32[1,16]{1,0:T(1,128)}, u32[]{:S(2)}) copy-start(s32[1,16]{1,0:T(1,128)} %send_ref.1) | copy-start | bytes 196
  1.9 2.8 %copy-start.4 = (bf16[256,1024]{1,0:T(8,128)(2,1)S(1)}, bf16[256,1024]{1,0:T(8,128)(2,1)}, u32[]{:S(2)}) copy-start(bf16[256,1024]{1,0:T(8,128)(2,1)} %feat_ref.3) | copy-start | bytes 1572868
  1.9 22.0 %copy-start = (bf16[1024,1024]{1,0:T(8,128)(2,1)S(1)}, bf16[1024,1024]{1,0:T(8,128)(2,1)}, u32[]{:S(2)}) copy-start(bf16[1024,1024]{1,0:T(8,128)(2,1)} %wk_ref.5) | copy-start | bytes 6291460
  1.9 22.0 %copy-start.1 = (bf16[1024,1024]{1,0:T(8,128)(2,1)S(1)}, bf16[1024,1024]{1,0:T(8,128)(2,1)}, u32[]{:S(2)}) copy-start(bf16[1024,1024]{1,0:T(8,128)(2,1)} %wv_ref.5) | copy-start | bytes 6291460
  1.9 22.0 %copy-start.5 = (bf16[1024,1024]{1,0:T(8,128)(2,1)S(1)}, bf16[1024,1024]{1,0:T(8,128)(2,1)}, u32[]{:S(2)}) copy-start(bf16[1024,1024]{1,0:T(8,128)(2,1)} %wq_ref.1) | copy-start | bytes 6291460
  2.6 8.7 %collective-permute-start.4 = (bf16[128,1024]{1,0:T(8,128)(2,1)S(1)}, bf16[128,1024]{1,0:T(8,128)(2,1)S(1)}, u32[]{:S(2)}, u32[]{:S(2)}) collective-permute-start(bf16[128,1024]{1,0:T(8,128)(2,1)S(1)} %get-tuple-element.43), channel_id=1, source_target_pairs={{0,64},{16,80},{32,96},{48,112},{64,128},{80,144},{96,160},{112,17... | collective-permute-start | bytes 786440 | tf_op jit(solution)/shard_map/ppermute | solution.py:393
  4.7 15.6 %collective-permute-start = (bf16[256,1024]{1,0:T(8,128)(2,1)S(1)}, bf16[256,1024]{1,0:T(8,128)(2,1)S(1)}, u32[]{:S(2)}, u32[]{:S(2)}) collective-permute-start(bf16[256,1024]{1,0:T(8,128)(2,1)S(1)} %copy-done.4), channel_id=1, source_target_pairs={{0,32},{16,48},{32,0},{48,16},{64,96},{80,112},{96,64},{112,80},{1... | collective-permute-start | bytes 1572872 | tf_op jit(solution)/shard_map/ppermute | solution.py:376
  7.6 12.7 %collective-permute-start.1 = (bf16[8,1024]{1,0:T(8,128)(2,1)S(1)}, bf16[8,1024]{1,0:T(8,128)(2,1)S(1)}, u32[]{:S(2)}, u32[]{:S(2)}) collective-permute-start(bf16[8,1024]{1,0:T(8,128)(2,1)S(1)} %get-tuple-element.39), channel_id=1, source_target_pairs={{0,32},{16,48},{32,0},{48,16},{64,96},{80,112},{96,64},{112,80},{1... | collective-permute-start | bytes 49160 | tf_op jit(solution)/shard_map/ppermute | solution.py:396
  7.6 10.8 %collective-permute-start.5 = (bf16[128,1024]{1,0:T(8,128)(2,1)S(1)}, bf16[128,1024]{1,0:T(8,128)(2,1)S(1)}, u32[]{:S(2)}, u32[]{:S(2)}) collective-permute-start(bf16[128,1024]{1,0:T(8,128)(2,1)S(1)} %get-tuple-element.44), channel_id=1, source_target_pairs={{0,128},{16,144},{32,160},{48,176},{64,192},{80,208},{96,224},{112... | collective-permute-start | bytes 786440 | tf_op jit(solution)/shard_map/ppermute | solution.py:393
  10.1 10.2 %collective-permute-start.6 = (bf16[128,1024]{1,0:T(8,128)(2,1)S(1)}, bf16[128,1024]{1,0:T(8,128)(2,1)S(1)}, u32[]{:S(2)}, u32[]{:S(2)}) collective-permute-start(bf16[128,1024]{1,0:T(8,128)(2,1)S(1)} %get-tuple-element.45), channel_id=1, source_target_pairs={{0,192},{16,208},{32,224},{48,240},{64,0},{80,16},{96,32},{112,48}... | collective-permute-start | bytes 786440 | tf_op jit(solution)/shard_map/ppermute | solution.py:393
  20.8 27.2 %collective-permute-start.7 = (bf16[320,1024]{1,0:T(8,128)(2,1)S(1)}, bf16[320,1024]{1,0:T(8,128)(2,1)S(1)}, u32[]{:S(2)}, u32[]{:S(2)}) collective-permute-start(bf16[320,1024]{1,0:T(8,128)(2,1)S(1)} %constant_dynamic-update-slice_fusion), channel_id=1, source_target_pairs={{0,16},{16,0},{32,48},{48,32},{64,80},{80,64},{96,112},{112,96},{1... | collective-permute-start | bytes 1966088 | tf_op jit(solution)/shard_map/ppermute | solution.py:426
  27.3 13.4 %collective-permute-start.8 = (bf16[128,1024]{1,0:T(8,128)(2,1)S(1)}, bf16[128,1024]{1,0:T(8,128)(2,1)S(1)}, u32[]{:S(2)}, u32[]{:S(2)}) collective-permute-start(bf16[128,1024]{1,0:T(8,128)(2,1)S(1)} %get-tuple-element.48), channel_id=1, source_target_pairs={{0,1},{1,2},{2,3},{3,4},{4,5},{5,6},{6,7},{7,8},{8,9},{9,10},{10,1... | collective-permute-start | bytes 786440 | tf_op jit(solution)/shard_map/ppermute | solution.py:415
  28.7 14.0 %collective-permute-start.9 = (bf16[128,1024]{1,0:T(8,128)(2,1)S(1)}, bf16[128,1024]{1,0:T(8,128)(2,1)S(1)}, u32[]{:S(2)}, u32[]{:S(2)}) collective-permute-start(bf16[128,1024]{1,0:T(8,128)(2,1)S(1)} %get-tuple-element.49), channel_id=1, source_target_pairs={{0,15},{1,0},{2,1},{3,2},{4,3},{5,4},{6,5},{7,6},{8,7},{9,8},{10,9... | collective-permute-start | bytes 786440 | tf_op jit(solution)/shard_map/ppermute | solution.py:416
  34.1 11.3 %collective-permute-start.2 = (bf16[64,1024]{1,0:T(8,128)(2,1)S(1)}, bf16[64,1024]{1,0:T(8,128)(2,1)S(1)}, u32[]{:S(2)}, u32[]{:S(2)}) collective-permute-start(bf16[64,1024]{1,0:T(8,128)(2,1)S(1)} %get-tuple-element.41), channel_id=1, source_target_pairs={{0,64},{16,80},{32,96},{48,112},{64,128},{80,144},{96,160},{112,17... | collective-permute-start | bytes 393224 | tf_op jit(solution)/shard_map/ppermute | solution.py:425
  35.5 10.7 %collective-permute-start.3 = (bf16[64,1024]{1,0:T(8,128)(2,1)S(1)}, bf16[64,1024]{1,0:T(8,128)(2,1)S(1)}, u32[]{:S(2)}, u32[]{:S(2)}) collective-permute-start(bf16[64,1024]{1,0:T(8,128)(2,1)S(1)} %get-tuple-element.42), channel_id=1, source_target_pairs={{0,192},{16,208},{32,224},{48,240},{64,0},{80,16},{96,32},{112,48}... | collective-permute-start | bytes 393224 | tf_op jit(solution)/shard_map/ppermute | solution.py:425
  40.7 11.5 %collective-permute-start.10 = (bf16[64,1024]{1,0:T(8,128)(2,1)S(1)}, bf16[64,1024]{1,0:T(8,128)(2,1)S(1)}, u32[]{:S(2)}, u32[]{:S(2)}) collective-permute-start(bf16[64,1024]{1,0:T(8,128)(2,1)S(1)} %get-tuple-element.52), channel_id=1, source_target_pairs={{0,80},{16,64},{32,112},{48,96},{64,144},{80,128},{96,176},{112,16... | collective-permute-start | bytes 393224 | tf_op jit(solution)/shard_map/ppermute | solution.py:425
  42.7 11.2 %collective-permute-start.11 = (bf16[64,1024]{1,0:T(8,128)(2,1)S(1)}, bf16[64,1024]{1,0:T(8,128)(2,1)S(1)}, u32[]{:S(2)}, u32[]{:S(2)}) collective-permute-start(bf16[64,1024]{1,0:T(8,128)(2,1)S(1)} %get-tuple-element.53), channel_id=1, source_target_pairs={{0,208},{16,192},{32,240},{48,224},{64,16},{80,0},{96,48},{112,32}... | collective-permute-start | bytes 393224 | tf_op jit(solution)/shard_map/ppermute | solution.py:425
  45.4 8.5 %collective-permute-start.12 = (bf16[64,1024]{1,0:T(8,128)(2,1)S(1)}, bf16[64,1024]{1,0:T(8,128)(2,1)S(1)}, u32[]{:S(2)}, u32[]{:S(2)}) collective-permute-start(bf16[64,1024]{1,0:T(8,128)(2,1)S(1)} %get-tuple-element.54), channel_id=1, source_target_pairs={{0,128},{16,144},{32,160},{48,176},{64,192},{80,208},{96,224},{112... | collective-permute-start | bytes 393224 | tf_op jit(solution)/shard_map/ppermute | solution.py:425
  46.2 8.7 %collective-permute-start.13 = (bf16[64,1024]{1,0:T(8,128)(2,1)S(1)}, bf16[64,1024]{1,0:T(8,128)(2,1)S(1)}, u32[]{:S(2)}, u32[]{:S(2)}) collective-permute-start(bf16[64,1024]{1,0:T(8,128)(2,1)S(1)} %get-tuple-element.55), channel_id=1, source_target_pairs={{0,144},{16,128},{32,176},{48,160},{64,208},{80,192},{96,240},{112... | collective-permute-start | bytes 393224 | tf_op jit(solution)/shard_map/ppermute | solution.py:425
  48.0 7.0 %copy-start.2 = (bf16[1024,1024]{1,0:T(8,128)(2,1)S(1)}, bf16[1024,1024]{1,0:T(8,128)(2,1)}, u32[]{:S(2)}) copy-start(bf16[1024,1024]{1,0:T(8,128)(2,1)} %wo_ref.1) | copy-start | bytes 6291460
  48.0 7.0 %copy-start.6 = (s32[2,6]{1,0:T(2,128)S(1)}, s32[2,6]{1,0:T(2,128)}, u32[]{:S(2)}) copy-start(s32[2,6]{1,0:T(2,128)} %peers_hbm.1) | copy-start | bytes 148
  48.0 7.0 %copy-start.7 = (s32[2]{0:T(128)S(1)}, s32[2]{0:T(128)}, u32[]{:S(2)}) copy-start(s32[2]{0:T(128)} %count_hbm.1) | copy-start | bytes 28
